TPU v7x, 32 devices: a whole 2x2x4 slice. The times are simulated.
32 devices in a mesh: dp: 4 (over y, x), mp: 8 (over z, core).
Axes of the slice: x: 2, y: 2, z: 4, core: 2. Of those that a mesh axis runs over, the one named last changes fastest.
Arguments:
- image: bfloat16 [4, 2048, 1280], P('dp', 'mp'), may hold values from -6 to 6
- ln_gain: float32 [1280], replicated, may hold values from 0.1 to 1.9
- fc1_weight: bfloat16 [1280, 5120], P(None, ('dp', 'mp')), may hold values from -0.15625 to 0.15625
- fc2_weight: bfloat16 [5120, 1280], P(('dp', 'mp')), may hold values from -0.078125 to 0.078125
- projector_weight: bfloat16 [1280, 8192], P(None, 'mp'), may hold values from -0.15625 to 0.15625
- kv_weight: bfloat16 [8192, 8, 2, 128], P('mp'), may hold values from -0.0625 to 0.0625
- text: bfloat16 [4, 128, 8192], P('dp'), may hold values from -480 to 480
- q_weight: bfloat16 [8192, 8192], P(None, 'mp'), may hold values from -0.0625 to 0.0625
- o_weight: bfloat16 [8192, 8192], P('mp'), may hold values from -0.0625 to 0.0625
- tile_count: int32 [4], P('dp'), may hold values from 1 to 4
- text_start: int32 [4], P('dp'), may hold values from 0 to 63
Outputs:
- attended: bfloat16 [4, 128, 8192], P('dp', 'mp')
All inputs are finite; a program needn't handle non-finite values.
Results may differ from a plain program's by a relative error of at most 0.035.
Values may be sent and summed in bfloat16 or wider, within the bound.
A program may use at most 128 MiB of HBM per device.

v0:
```python
import functools

import jax
import jax.numpy as jnp
from jax import lax
from jax.experimental import pallas as pl
from jax.experimental.pallas import tpu as pltpu
from jax.sharding import PartitionSpec as P

HEAD_DIM = 128
TILE_TOK = 512

MESH = pl.DeviceIdType.MESH
CORES = 2


def count_copies(kind):
    name, axis = kind
    size = lax.axis_size(axis)
    if name == "chain":
        return 2 * (size // CORES - 1) + size // CORES
    if name == "partner":
        return size // CORES
    if name == "stride":
        return size // CORES - 1
    return size - 1


def exchange_kernel(kinds, *refs):
    count = len(kinds)
    sources, results = refs[:count], refs[count : 2 * count]
    local_sem = refs[2 * count]
    sends, recvs = refs[2 * count + 1 : 3 * count + 1], refs[3 * count + 1 :]
    axes = sorted({axis for _, axis in kinds})

    barrier = pltpu.get_barrier_semaphore()
    greeted = 0
    for axis in axes:
        size, me = lax.axis_size(axis), lax.axis_index(axis)
        for step in range(1, size):
            pl.semaphore_signal(
                barrier, inc=1, device_id={axis: lax.rem(me + step, size)}, device_id_type=MESH
            )
        greeted += size - 1
    pl.semaphore_wait(barrier, greeted)

    def remote(op, source, result, slot, axis, peer):
        return pltpu.make_async_remote_copy(
            src_ref=source,
            dst_ref=result,
            send_sem=sends[op].at[slot],
            recv_sem=recvs[op].at[slot],
            device_id={axis: peer},
            device_id_type=MESH,
        )

    simple, chains, locals_ = [], [], []
    for op, (name, axis) in enumerate(kinds):
        size, me = lax.axis_size(axis), lax.axis_index(axis)
        source, result = sources[op], results[op]
        core = lax.rem(me, CORES)
        spot = lax.div(me, CORES)
        partner = me + 1 - 2 * core
        if name == "gather":
            for step in range(1, size):
                copy = remote(op, source, result.at[me], step - 1, axis, lax.rem(me + step, size))
                copy.start()
                simple.append(copy)
            locals_.append(pltpu.make_async_copy(source, result.at[me], local_sem.at[op]))
        elif name == "columns":
            width = result.shape[-1]

            def column(index):
                return source.at[:, pl.ds(pl.multiple_of(index * width, width), width)]

            for step in range(1, size):
                peer = lax.rem(me + step, size)
                copy = remote(op, column(peer), result.at[me], step - 1, axis, peer)
                copy.start()
                simple.append(copy)
            locals_.append(pltpu.make_async_copy(column(me), result.at[me], local_sem.at[op]))
        elif name == "scatter":
            for step in range(1, size):
                peer = lax.rem(me + step, size)
                copy = remote(op, source.at[peer], result.at[me], step - 1, axis, peer)
                copy.start()
                simple.append(copy)
            locals_.append(pltpu.make_async_copy(source.at[me], result.at[me], local_sem.at[op]))
        elif name == "partner":
            for chip in range(size // CORES):
                copy = remote(
                    op, source.at[chip * CORES + 1 - core], result.at[chip], chip, axis, partner
                )
                copy.start()
                simple.append(copy)
        elif name == "stride":
            chips = size // CORES
            for step in range(1, chips):
                other = lax.rem(spot + step, chips)
                copy = remote(
                    op, source.at[other], result.at[spot], step - 1, axis, other * CORES + core
                )
                copy.start()
                simple.append(copy)
            locals_.append(pltpu.make_async_copy(source.at[spot], result.at[spot], local_sem.at[op]))
        else:
            chains.append((op, axis, size // CORES, me, core, spot, partner, source, result))
    for copy in locals_:
        copy.start()

    def hop(chain, source, block, slot, peer):
        op, axis, result = chain[0], chain[1], chain[-1]
        return remote(op, source, result.at[block], slot, axis, peer)

    for chain in chains:
        op, axis, chips, me, core, spot, partner, source, result = chain

        @pl.when(spot + 1 < chips)
        def _():
            hop(chain, source, me, 0, me + CORES).start()

        @pl.when(spot > 0)
        def _():
            hop(chain, source, me, chips - 1, me - CORES).start()

    for chain in chains:
        op, axis, chips, me, core, spot, partner, source, result = chain
        hop(chain, source, me, 2 * (chips - 1), partner).start()
        pltpu.make_async_copy(source, result.at[me], local_sem.at[op]).start()
    for step in range(1, max([chain[2] for chain in chains], default=0)):
        for chain in chains:
            op, axis, chips, me, core, spot, partner, source, result = chain
            for sign, base in ((1, 0), (-1, chips - 1)):
                origin_spot = spot - sign * step
                here = (origin_spot >= 0) & (origin_spot < chips)
                onward = (spot + sign >= 0) & (spot + sign < chips)
                block = me - sign * step * CORES

                @pl.when(here)
                def _():
                    held = result.at[block]
                    hop(chain, held, block, base + step - 1, me).wait_recv()

                    @pl.when(onward)
                    def _():
                        hop(chain, held, block, base + step, me + sign * CORES).start()

                    slot = 2 * (chips - 1) + lax.rem(origin_spot - spot + chips, chips)
                    hop(chain, held, block, slot, partner).start()

    for chain in chains:
        op, axis, chips, me, core, spot, partner, source, result = chain
        for step in range(chips):
            for_spot = lax.rem(spot + step, chips)
            block = for_spot * CORES + core
            theirs = for_spot * CORES + 1 - core
            slot = 2 * (chips - 1) + step
            hop(chain, result.at[block], block, slot, partner).wait_send()
            hop(chain, result.at[theirs], theirs, slot, partner).wait_recv()
        for step in range(chips - 1):
            for sign, base in ((1, 0), (-1, chips - 1)):
                origin_spot = spot - sign * step
                sent = (
                    (origin_spot >= 0)
                    & (origin_spot < chips)
                    & (spot + sign >= 0)
                    & (spot + sign < chips)
                )
                block = me - sign * step * CORES

                @pl.when(sent)
                def _():
                    hop(chain, source, block, base + step, partner).wait_send()

        pltpu.make_async_copy(source, result.at[me], local_sem.at[op]).wait()
    for copy in simple:
        copy.wait()
    for copy in locals_:
        copy.wait()


def exchange(kinds, arrays, number):
    kinds = tuple(kinds)
    shapes = []
    for (name, axis), array in zip(kinds, arrays):
        size = lax.axis_size(axis)
        if name in ("gather", "chain"):
            shape = (size,) + array.shape
        elif name == "columns":
            shape = (size, array.shape[0], array.shape[1] // size)
        elif name == "scatter":
            shape = array.shape
        else:
            shape = (size // CORES,) + array.shape[1:]
        shapes.append(jax.ShapeDtypeStruct(shape, array.dtype))
    sems = [pltpu.SemaphoreType.DMA((count_copies(kind),)) for kind in kinds]
    return pl.pallas_call(
        functools.partial(exchange_kernel, kinds),
        out_shape=shapes,
        in_specs=[pl.BlockSpec(memory_space=pl.ANY)] * len(kinds),
        out_specs=[pl.BlockSpec(memory_space=pl.ANY)] * len(kinds),
        scratch_shapes=[pltpu.SemaphoreType.DMA((len(kinds),))] + sems + sems,
        compiler_params=pltpu.CompilerParams(collective_id=number, has_side_effects=True),
        name="exchange",
    )(*arrays)


def swapped(block, axis, bit):
    count = lax.axis_size(axis)
    route = []
    for low in range(count):
        high = low | 1 << bit
        if high != low and high < count:
            route += [(low, high), (high, low)]
    return lax.ppermute(block, axis, route)


def layer_norm(values, gain):
    center = values - jnp.mean(values, axis=-1, keepdims=True)
    spread = jnp.mean(center * center, axis=-1, keepdims=True)
    return center * lax.rsqrt(spread + 1e-05) * gain


def attend_block(block_queries, keys, values, valid, scale, layout):
    scores = (
        jnp.einsum(
            "thd," + layout + "->htk", block_queries, keys, preferred_element_type=jnp.float32
        )
        * scale
    )
    scores = jnp.where(valid[None, None, :], scores, -1e30)
    top = jnp.max(scores, axis=-1, keepdims=True)
    weights = jnp.exp(scores - top)
    probs = (weights / jnp.sum(weights, axis=-1, keepdims=True)).astype(jnp.bfloat16)
    return jnp.einsum("htk," + layout + "->thd", probs, values, preferred_element_type=jnp.float32)


def local(
    image,
    ln_gain,
    fc1_weight,
    fc2_weight,
    projector_weight,
    kv_weight,
    text,
    q_weight,
    o_weight,
    tile_count,
    text_start,
):
    inputs = image[0].astype(jnp.float32)
    group_count = lax.axis_size("mp")
    normed = layer_norm(inputs, ln_gain).astype(jnp.bfloat16)
    up, down, all_normed = exchange(
        (("chain", "mp"), ("chain", "mp"), ("gather", "dp")), (fc1_weight.T, fc2_weight, normed), 0
    )
    up = up.reshape(-1, up.shape[-1])
    down = down.reshape(-1, down.shape[-1])
    all_normed = all_normed.reshape(-1, all_normed.shape[-1])
    hidden = jax.nn.gelu(
        lax.dot_general(
            all_normed, up, (((1,), (1,)), ((), ())), preferred_element_type=jnp.float32
        ),
        approximate=False,
    ).astype(jnp.bfloat16)
    branch = jnp.dot(hidden, down, preferred_element_type=jnp.float32).astype(jnp.bfloat16)
    branch = branch.reshape((lax.axis_size("dp"),) + inputs.shape)

    kv_count = kv_weight.shape[1]
    devices_per_kv = group_count // kv_count
    kv_columns = kv_count * 2 * HEAD_DIM
    flat_kv = kv_weight.reshape(kv_weight.shape[0], kv_columns)
    row_count = projector_weight.shape[0] // lax.axis_size("dp")
    rows = lax.dynamic_slice_in_dim(
        projector_weight, lax.axis_index("dp") * row_count, row_count, axis=0
    )
    folded = jnp.dot(rows, flat_kv, preferred_element_type=jnp.float32).astype(jnp.bfloat16)
    terms, folded = exchange((("scatter", "dp"), ("columns", "mp")), (branch, folded), 1)
    encoded = (inputs + jnp.sum(terms.astype(jnp.float32), axis=0)).astype(jnp.bfloat16)
    folded = jnp.sum(folded.astype(jnp.float32), axis=0).astype(jnp.bfloat16)
    for bit_index in range(devices_per_kv.bit_length() - 1):
        partner = swapped(folded, "mp", bit_index)
        is_lower = lax.axis_index("mp") // (1 << bit_index) % 2 == 0
        folded = jnp.where(
            is_lower, jnp.concatenate([folded, partner], 1), jnp.concatenate([partner, folded], 1)
        )
    all_encoded, folded = exchange((("chain", "mp"), ("gather", "dp")), (encoded, folded), 2)
    all_encoded = all_encoded.reshape(-1, all_encoded.shape[-1])
    folded = folded.reshape(-1, folded.shape[-1])
    image_rows = all_encoded.shape[0]
    portion = jnp.einsum("rc,kr->ck", folded, all_encoded, preferred_element_type=jnp.float32)
    keys = portion[:HEAD_DIM]
    key_scale = lax.rsqrt(jnp.mean(keys * keys, axis=0, keepdims=True) + 1e-06)
    keys = (keys * key_scale).astype(jnp.bfloat16)
    values = portion[HEAD_DIM:].astype(jnp.bfloat16)
    layout = "dk"
    text_rows = text.shape[1]
    local_heads = q_weight.shape[1] // HEAD_DIM
    queries = jnp.dot(text[0], q_weight, preferred_element_type=jnp.float32).astype(jnp.bfloat16)
    queries = queries.reshape(text_rows, local_heads, HEAD_DIM)
    valid = jnp.arange(image_rows, dtype=jnp.int32) // TILE_TOK < tile_count[0]
    scale = 1.0 / HEAD_DIM**0.5
    block_rows = min(text_rows, 256)
    blocks = queries.reshape(text_rows // block_rows, block_rows, local_heads, HEAD_DIM)
    attended_heads = lax.map(
        lambda block_queries: attend_block(block_queries, keys, values, valid, scale, layout),
        blocks,
    )
    attended_heads = attended_heads.reshape(text_rows, local_heads * HEAD_DIM)
    row_mask = (jnp.arange(text_rows, dtype=jnp.int32) >= text_start[0]).astype(jnp.float32)
    heads_out = (attended_heads * row_mask[:, None]).astype(jnp.bfloat16)
    out = jnp.dot(heads_out, o_weight, preferred_element_type=jnp.float32).astype(jnp.bfloat16)
    out = out.reshape(group_count, text_rows // group_count, out.shape[-1])
    (theirs,) = exchange((("partner", "mp"),), (out,), 3)
    chip_out = out.reshape((group_count // CORES, CORES) + out.shape[1:])
    mine = lax.dynamic_index_in_dim(
        chip_out, lax.axis_index("mp") % CORES, axis=1, keepdims=False
    )
    paired = (mine.astype(jnp.float32) + theirs.astype(jnp.float32)).astype(jnp.bfloat16)
    (terms,) = exchange((("stride", "mp"),), (paired,), 4)
    summed_out = jnp.sum(terms.astype(jnp.float32), axis=0).astype(jnp.bfloat16)
    return summed_out[None]


def solution(mesh):
    return jax.shard_map(
        local,
        mesh=mesh,
        in_specs=(
            P("dp", "mp", None),
            P(),
            P(None, ("dp", "mp")),
            P(("dp", "mp"), None),
            P(None, "mp"),
            P("mp", None, None, None),
            P("dp", None, None),
            P(None, "mp"),
            P("mp", None),
            P("dp"),
            P("dp"),
        ),
        out_specs=P("dp", "mp", None),
        check_vma=False,
    )
```

profile of v0, /device:TPU:0, one launch (start us, length us, event | category | flops | bytes accessed | tf_op | source)
XLA Modules:
  0.0 258.9 jit_solution(10231856760635636548)
XLA Ops:
  0.0 0.0 copy-start
  0.0 1.4 convert_reduce_fusion.1
  1.4 1.4 fusion.56
  2.8 2.2 fusion.58.refs_2_
  5.0 61.8 %exchange.5 = (bf16[8,160,1280]{2,1,0:T(8,128)(2,1)}, bf16[8,160,1280]{2,1,0:T(8,128)(2,1)}, bf16[4,256,1280]{2,1,0:T(8,128)(2,1)}) custom-call(bf16[160,1280]{1,0:T(8,128)(2,1)} %bitcast.101, bf16[160,1280]{1,0:T(8,128)(2,1)} %refs_1_.1, bf16[256,1280]{1,0:T(8,128)(2,1)} %fusion.58.refs_2_), custom_call_target="tpu_custom_call" | custom-call | tf_op jit(solution)/shard_map/exchange/pallas_call | solution.py:197
  66.8 21.3 %convolution_convert_fusion.1 = bf16[1024,1280]{1,0:T(8,128)(2,1)} fusion(bf16[1280,1280]{1,0:T(8,128)(2,1)} %bitcast.104, bf16[1024,1280]{1,0:T(8,128)(2,1)} %bitcast.105, bf16[1280,1280]{1,0:T(8,128)(2,1)} %bitcast.103), kind=kOutput, calls=%fused_computation.32 | convolution fusion | flops 6797393920 | bytes 11796480 | tf_op jit(solution)/shard_map/dot_general | solution.py:266
  88.1 7.8 %reshape.78 = bf16[1024,2048]{1,0:T(8,128)(2,1)} reshape(bf16[1024,8,2,128]{3,2,1,0:T(2,128)(2,1)} %param.16) | data formatting | bytes 8388608 | tf_op jit(solution)/shard_map/reshape | solution.py:272
  95.9 0.0 copy-done
  95.9 4.8 %convolution_convert_fusion.2.refs_1_ = bf16[320,2048]{1,0:T(8,128)(2,1)} fusion(bf16[1024,2048]{1,0:T(8,128)(2,1)} %reshape.78, bf16[1280,1024]{1,0:T(8,128)(2,1)S(1)} %copy-done, s32[]{:T(128)S(6)} %select_n.31), kind=kOutput, calls=%fused_computation.33 | convolution fusion | flops 1342832640 | bytes 6160388 | tf_op jit(solution)/shard_map/dot_general | solution.py:277
  100.7 0.0 copy-start.2
  100.7 32.6 %exchange.6 = (bf16[4,256,1280]{2,1,0:T(8,128)(2,1)}, bf16[8,320,256]{2,1,0:T(8,128)(2,1)}) custom-call(bf16[4,256,1280]{2,1,0:T(8,128)(2,1)} %bitcast.100, bf16[320,2048]{1,0:T(8,128)(2,1)} %convolution_convert_fusion.2.refs_1_), custom_call_target="tpu_custom_call" | custom-call | tf_op jit(solution)/shard_map/exchange/pallas_call | solution.py:197
  133.3 2.2 convert_reduce_fusion
  135.6 0.0 copy-done.2
  135.6 1.0 fusion.59.refs_0_
  136.5 2.2 reduce_sum.73.refs_1_
  138.7 0.0 copy-start.3
  138.7 51.5 %exchange.7 = (bf16[8,256,1280]{2,1,0:T(8,128)(2,1)}, bf16[4,320,256]{2,1,0:T(8,128)(2,1)}) custom-call(bf16[256,1280]{1,0:T(8,128)(2,1)} %fusion.59.refs_0_, bf16[320,256]{1,0:T(8,128)(2,1)} %reduce_sum.73.refs_1_), custom_call_target="tpu_custom_call" | custom-call | tf_op jit(solution)/shard_map/exchange/pallas_call | solution.py:197
  190.2 4.3 %fusion.136 = f32[256,2048]{1,0:T(8,128)S(1)} fusion(bf16[1280,256]{1,0:T(8,128)(2,1)} %bitcast.106, bf16[2048,1280]{1,0:T(8,128)(2,1)} %bitcast.102), kind=kOutput, calls=%fused_computation.140 | convolution fusion | flops 1342177280 | bytes 7995392 | tf_op jit(solution)/shard_map/rc,kr->ck/dot_general | solution.py:291
  194.5 0.0 copy-start.4
  194.5 1.4 copy-done.4
  195.9 0.1 multiply_reduce_fusion
  196.0 0.0 copy-done.3
  196.0 8.1 %fusion.63 = bf16[16,8,8,128]{3,2,1,0:T(8,128)(2,1)S(1)} fusion(bf16[8192,1024]{1,0:T(8,128)(2,1)} %param.18, bf16[1,128,8192]{2,1,0:T(8,128)(2,1)S(1)} %copy-done.3), kind=kOutput, calls=%fused_computation.78 | convolution fusion | flops 2147614720 | bytes 19136512 | tf_op jit(solution)/shard_map/dot_general | solution.py:299
  204.8 0.0 copy-start.5
  204.8 7.7 %fusion.125 = (f32[8,128]{1,0:T(8,128)S(1)}, f32[8,128,2048]{1,2,0:T(8,128)}) fusion(pred[2048]{0:T(1024)(128)(4,1)S(1)} %fusion.88, bf16[16,8,8,128]{3,2,1,0:T(8,128)(2,1)S(1)} %fusion.63, f32[256,2048]{1,0:T(8,128)} %copy-done.4, f32[2048]{0:T(1024)S(1)} %add_rsqrt_fusion), kind=kOutput, calls=%fused_computation.138 | convolution fusion | flops 545785856 | bytes 9713664 | tf_op jit(solution)/shard_map/while/body/eval_jaxpr/sub | solution.py:233
  212.5 0.0 copy-done.5
  212.5 4.1 %fusion.18 = f32[128,8,128]{2,0,1:T(8,128)S(1)} fusion(f32[8,128,2048]{1,2,0:T(8,128)} %get-tuple-element.38, f32[8,128]{1,0:T(8,128)S(1)} %get-tuple-element.37, f32[256,2048]{1,0:T(8,128)S(1)} %copy-done.5), kind=kOutput, calls=%fused_computation.31 | convolution fusion | flops 541065216 | bytes 9441280 | tf_op jit(solution)/shard_map/while/body/eval_jaxpr/htk,dk->thd/dot_general | solution.py:235
  217.3 0.0 copy-start.1
  217.3 9.7 %convolution_convert_fusion = bf16[128,8192]{1,0:T(8,128)(2,1)} fusion(bf16[128,1024]{0,1:T(8,128)(2,1)S(1)} %fusion.72, bf16[1024,8192]{1,0:T(8,128)(2,1)} %param.19), kind=kOutput, calls=%fused_computation.1 | convolution fusion | flops 2148532224 | bytes 19136512 | tf_op jit(solution)/shard_map/dot_general | solution.py:312
  227.1 5.1 %exchange.8 = bf16[4,16,8192]{2,1,0:T(8,128)(2,1)} custom-call(bf16[8,16,8192]{2,1,0:T(8,128)(2,1)} %bitcast.98), custom_call_target="tpu_custom_call" | custom-call | tf_op jit(solution)/shard_map/exchange/pallas_call | solution.py:197
  232.2 2.8 %fusion.49.refs_0_ = bf16[4,16,8192]{2,1,0:T(8,128)(2,1)} fusion(bf16[4,16,8192]{2,1,0:T(8,128)(2,1)} %exchange.8, bf16[4,2,16,8192]{3,2,1,0:T(8,128)(2,1)} %bitcast.99, s32[]{:T(128)S(6)} %select_n.36), kind=kLoop, calls=%fused_computation.64 | loop fusion | flops 2097152 | bytes 3145732 | tf_op jit(solution)/shard_map/convert_element_type | solution.py:319
  235.0 21.7 %exchange.9 = bf16[4,16,8192]{2,1,0:T(8,128)(2,1)} custom-call(bf16[4,16,8192]{2,1,0:T(8,128)(2,1)} %fusion.49.refs_0_), custom_call_target="tpu_custom_call" | custom-call | tf_op jit(solution)/shard_map/exchange/pallas_call | solution.py:197
  256.7 2.2 reduce_sum.76
  258.9 0.0 copy-done.1
  (6 shorter events, 0.1 us)
Async XLA Ops:
  0.0 95.9 %copy-start = (bf16[1280,1024]{1,0:T(8,128)(2,1)S(1)}, bf16[1280,1024]{1,0:T(8,128)(2,1)}, u32[]{:S(2)}) copy-start(bf16[1280,1024]{1,0:T(8,128)(2,1)} %param.15) | copy-start | bytes 7864324
  100.7 34.9 %copy-start.2 = (bf16[1,256,1280]{2,1,0:T(8,128)(2,1)S(1)}, bf16[1,256,1280]{2,1,0:T(8,128)(2,1)}, u32[]{:S(2)}) copy-start(bf16[1,256,1280]{2,1,0:T(8,128)(2,1)} %param.11) | copy-start | bytes 1966084
  138.7 57.3 %copy-start.3 = (bf16[1,128,8192]{2,1,0:T(8,128)(2,1)S(1)}, bf16[1,128,8192]{2,1,0:T(8,128)(2,1)}, u32[]{:S(2)}) copy-start(bf16[1,128,8192]{2,1,0:T(8,128)(2,1)} %param.17) | copy-start | bytes 6291460
  194.5 1.4 copy-start.4
  204.8 7.7 %copy-start.5 = (f32[256,2048]{1,0:T(8,128)S(1)}, f32[256,2048]{1,0:T(8,128)}, u32[]{:S(2)}) copy-start(f32[256,2048]{1,0:T(8,128)} %copy-done.4) | copy-start | bytes 6291460
  217.3 41.5 %copy-start.1 = (bf16[1280,1024]{1,0:T(8,128)(2,1)S(1)}, bf16[1280,1024]{1,0:T(8,128)(2,1)}, u32[]{:S(2)}) copy-start(bf16[1280,1024]{1,0:T(8,128)(2,1)} %param.15) | copy-start | bytes 7864324
where the time goes:
time: 262 us; the launch traced here: 259 us
  Pallas kernels  173 us (66%)
  matrix products  60 us (23%)
  other arithmetic  15.5 us (6%)
  local copies, waits for them, and re-layouts  9.2 us (4%)
    pallas_call x5, Pallas kernels, exchange(): pl.pallas_call(functools.partial(exchange_kernel, kinds), out_shape=shape...  173 us
    dot_general x1, matrix products, local(): jnp.dot(hidden, down, preferred_element_type=jnp.float32)  21.3 us
    dot_general x1, matrix products, local(): jnp.dot(heads_out, o_weight, preferred_element_type=jnp.float32)  9.74 us
    dot_general x1, matrix products, local(): jnp.dot(text[0], q_weight, preferred_element_type=jnp.float32)  8.1 us
    reshape x1, local copies, waits for them, and re-layouts, local(): flat_kv = kv_weight.reshape(kv_weight.shape[0], kv_columns)  7.79 us
    sub x1, matrix products, attend_block(): weights = jnp.exp(scores - top)  7.71 us

commit v1 on v0

--- a/solution.py
+++ b/solution.py
@@ -322,9 +322,627 @@
     return summed_out[None]
 
 
+def erf_gelu(values):
+    return 0.5 * values * (1.0 + lax.erf(values * 0.5**0.5))
+
+
+def fused_kernel(
+    image,
+    gain,
+    fc1,
+    fc2,
+    projector,
+    kv,
+    text,
+    q_weight,
+    o_weight,
+    tile_count,
+    text_start,
+    out,
+    up,
+    down,
+    pixels,
+    normed,
+    total,
+    x_send,
+    x_recv,
+    z_send,
+    z_recv,
+    encoded,
+    rows_part,
+    fold_part,
+    fold_0,
+    fold_1,
+    fold_2,
+    fold_3,
+    fold_4,
+    fold_own,
+    folded,
+    words,
+    staged,
+    q_total,
+    queries,
+    keys,
+    values,
+    mixed,
+    tops,
+    sums,
+    heads,
+    o_part,
+    o_0,
+    o_1,
+    o_2,
+    o_3,
+    o_4,
+    local_sem,
+    stage_sem,
+    sends,
+    recvs,
+):
+    dp, mp = lax.axis_index("dp"), lax.axis_index("mp")
+    core, spot = lax.rem(mp, CORES), lax.div(mp, CORES)
+    low, high = lax.rem(spot, 2), lax.div(spot, 2)
+    spot_1 = spot + 1 - 2 * low
+    spot_2 = spot + 2 - 4 * high
+    spot_3 = spot_1 + 2 - 4 * high
+    dp_x = dp + 1 - 2 * lax.rem(dp, 2)
+    dp_y = dp + 2 - 4 * lax.div(dp, 2)
+    pc = {"mp": spot * CORES + 1 - core}
+    x1, y1 = {"dp": dp_x}, {"dp": dp_y}
+    z1 = {"mp": spot_1 * CORES + core}
+    z2 = {"mp": spot_2 * CORES + core}
+
+    barrier = pltpu.get_barrier_semaphore()
+    for peer in (pc, x1, y1, z1, z2):
+        pl.semaphore_signal(barrier, inc=1, device_id=peer, device_id_type=MESH)
+
+    locals_ = []
+
+    def local(source, target):
+        copy = pltpu.make_async_copy(source, target, local_sem.at[len(locals_)])
+        copy.start()
+        locals_.append(copy)
+        return copy
+
+    rows = image.shape[0]
+    hidden = fc1.shape[0]
+    part_rows = rows_part.shape[0]
+    depth = staged.shape[1]
+    stages = staged.shape[0]
+    half = rows // 2
+
+    kv_parts = kv.shape[1] // depth
+    kv_copies = [
+        local(kv.at[:, pl.ds(i * depth, depth)], staged.at[i]) for i in range(kv_parts)
+    ]
+    part_copy = local(
+        projector.at[pl.ds(pl.multiple_of(dp * part_rows, part_rows), part_rows)], rows_part
+    )
+
+    def q_copy(step):
+        slot = lax.rem(step + kv_parts, stages)
+        return pltpu.make_async_copy(
+            q_weight.at[pl.ds(pl.multiple_of(step * depth, depth), depth)],
+            staged.at[slot],
+            stage_sem.at[slot],
+        )
+
+    def o_copy(step):
+        slot = lax.rem(step, stages)
+        return pltpu.make_async_copy(
+            o_weight.at[:, pl.ds(pl.multiple_of(step * depth, depth), depth)],
+            staged.at[slot],
+            stage_sem.at[slot],
+        )
+
+    text_copy = local(text, words)
+    for step in range(stages - kv_parts):
+        q_copy(step).start()
+    image_copy = local(image, pixels.at[0])
+    up_copy = local(fc1, up.at[0, pl.ds(0, hidden)])
+    down_copy = local(fc2, down.at[0, pl.ds(0, hidden)])
+
+    pl.semaphore_wait(barrier, 5)
+
+    started = []
+
+    def remote(source, target, peer):
+        slot = len(started)
+        copy = pltpu.make_async_remote_copy(
+            src_ref=source,
+            dst_ref=target,
+            send_sem=sends.at[slot],
+            recv_sem=recvs.at[slot],
+            device_id=peer,
+            device_id_type=MESH,
+        )
+        copy.start()
+        started.append(copy)
+        return copy
+
+    mine, theirs = pl.ds(0, hidden), pl.ds(hidden, hidden)
+    image_z = remote(image, pixels.at[2], z1)
+    image_x = remote(image, pixels.at[1], x1)
+    up_z = remote(fc1, up.at[2, mine], z2)
+    down_z = remote(fc2, down.at[2, mine], z2)
+    up_y = remote(fc1, up.at[1, mine], y1)
+    down_y = remote(fc2, down.at[1, mine], y1)
+    up_p = [remote(fc1, up.at[0, theirs], pc)]
+    down_p = [remote(fc2, down.at[0, theirs], pc)]
+
+    for copy in kv_copies:
+        copy.wait()
+    part_copy.wait()
+    columns = fold_part.shape[-1]
+    per_stage = depth // columns
+
+    def fold_step(head, carry):
+        start = pl.multiple_of(lax.rem(head, per_stage) * columns, columns)
+        block = staged[lax.div(head, per_stage), :, pl.ds(start, columns)]
+        fold_part[lax.div(head, CORES), lax.rem(head, CORES)] = jnp.dot(
+            rows_part[...], block, preferred_element_type=jnp.float32
+        ).astype(jnp.bfloat16)
+        return carry
+
+    lax.fori_loop(0, fold_part.shape[0] * CORES, fold_step, 0)
+    fold_p = remote(fold_part.at[:, 1 - core], fold_0, pc)
+    for step in range(stages - kv_parts, stages):
+        q_copy(step).start()
+
+    text_copy.wait()
+    q_steps = q_weight.shape[0] // depth
+    q_total[...] = jnp.zeros_like(q_total)
+
+    def q_step(step, carry):
+        q_copy(step).wait()
+        slot = lax.rem(step + kv_parts, stages)
+        q_total[...] += jnp.dot(
+            words[:, pl.ds(pl.multiple_of(step * depth, depth), depth)],
+            staged[slot],
+            preferred_element_type=jnp.float32,
+        )
+
+        @pl.when(step + stages < q_steps)
+        def _():
+            q_copy(step + stages).start()
+
+        return carry
+
+    lax.fori_loop(0, q_steps, q_step, 0)
+    text_rows = words.shape[0]
+    head_count = q_total.shape[1] // HEAD_DIM
+    for head in range(head_count):
+        queries[head // 2, pl.ds(head % 2 * text_rows, text_rows)] = q_total[
+            :, head * HEAD_DIM : (head + 1) * HEAD_DIM
+        ].astype(jnp.bfloat16)
+    for step in range(stages):
+        o_copy(step).start()
+
+    strip = 32
+
+    def normalise(block):
+        def one(step, carry):
+            spot_rows = pl.ds(pl.multiple_of(step * strip, strip), strip)
+            entry = pixels[block, spot_rows].astype(jnp.float32)
+            normed[block, spot_rows] = layer_norm(entry, gain[...]).astype(jnp.bfloat16)
+            return carry
+
+        lax.fori_loop(0, rows // strip, one, 0)
+
+    tile = 256
+
+    def mlp(block, first, last, base, stride=1):
+        def one(step, carry):
+            row = base + step * stride
+            inner = lax.dot_general(
+                normed[row], up[block], (((1,), (1,)), ((), ())), preferred_element_type=jnp.float32
+            )
+            inner = erf_gelu(inner).astype(jnp.bfloat16)
+            for begin in range(0, total.shape[-1], tile):
+                area = pl.ds(begin, tile)
+                term = jnp.dot(inner, down[block, :, area], preferred_element_type=jnp.float32)
+                if first:
+                    total[row, :, area] = term
+                else:
+                    total[row, :, area] += term
+            return carry
+
+        lax.fori_loop(0, last, one, 0)
+
+    image_copy.wait()
+    up_copy.wait()
+    down_copy.wait()
+    normalise(0)
+    up_p[0].wait_recv()
+    down_p[0].wait_recv()
+    mlp(0, True, 1, 0)
+    image_z.wait_recv()
+    image_d = remote(pixels.at[2], pixels.at[3], x1)
+    normalise(2)
+    fold_p.wait_recv()
+    spots = fold_0.shape[0]
+
+    def fold_pair(index, carry):
+        fold_1[lax.div(index, 2), lax.rem(index, 2)] = (
+            fold_part[index, core].astype(jnp.float32) + fold_0[index].astype(jnp.float32)
+        ).astype(jnp.bfloat16)
+        return carry
+
+    lax.fori_loop(0, spots, fold_pair, 0)
+    image_x.wait_recv()
+    normalise(1)
+    mlp(0, True, 2, 1)
+
+    up_z.wait_recv()
+    up_d = remote(up.at[2, mine], up.at[3, mine], y1)
+    up_p.append(remote(up.at[2, mine], up.at[2, theirs], pc))
+    up_y.wait_recv()
+    up_p.append(remote(up.at[1, mine], up.at[1, theirs], pc))
+    down_y.wait_recv()
+    down_p.append(remote(down.at[1, mine], down.at[1, theirs], pc))
+    image_d.wait_recv()
+    normalise(3)
+    mlp(0, True, 1, 3)
+    down_z.wait_recv()
+    down_d = remote(down.at[2, mine], down.at[3, mine], y1)
+    down_p.append(remote(down.at[2, mine], down.at[2, theirs], pc))
+    fold_z = remote(fold_1.at[:, 1 - low], fold_2, z1)
+    up_p[2].wait_recv()
+    down_p[1].wait_recv()
+    mlp(1, False, 4, 0)
+    up_p[1].wait_recv()
+    down_p[2].wait_recv()
+    mlp(2, False, 4, 0)
+    fold_z.wait_recv()
+    for index in range(2):
+        fold_3[index] = (
+            fold_1[index, low].astype(jnp.float32) + fold_2[index].astype(jnp.float32)
+        ).astype(jnp.bfloat16)
+    fold_zz = remote(fold_3.at[1 - high], fold_4, z2)
+    up_d.wait_recv()
+    up_p.append(remote(up.at[3, mine], up.at[3, theirs], pc))
+    fold_zz.wait_recv()
+    fold_own[...] = (
+        fold_3[high].astype(jnp.float32) + fold_4[...].astype(jnp.float32)
+    ).astype(jnp.bfloat16)
+
+    def fold_rows(owner):
+        return folded.at[pl.ds(pl.multiple_of(owner * part_rows, part_rows), part_rows)]
+
+    fold_local = local(fold_own, fold_rows(dp))
+    fold_x = remote(fold_own, fold_rows(dp), x1)
+    fold_y = remote(fold_own, fold_rows(dp), y1)
+    down_d.wait_recv()
+    down_p.append(remote(down.at[3, mine], down.at[3, theirs], pc))
+    up_p[3].wait_recv()
+    down_p[3].wait_recv()
+
+    def to_x(row, part):
+        index = row // 2
+        x_send[index, part] = total[row, pl.ds(part * half, half)].astype(jnp.bfloat16)
+        return remote(x_send.at[index, part], x_recv.at[index, part], x1)
+
+    mlp(3, False, 1, 1)
+    x_copies = {(0, 0): to_x(1, 0)}
+    mlp(3, False, 1, 3)
+    x_copies[1, 0] = to_x(3, 0)
+    x_copies[0, 1] = to_x(1, 1)
+    x_copies[1, 1] = to_x(3, 1)
+    mlp(3, False, 2, 0, 2)
+    fold_x.wait_recv()
+    fold_d = remote(fold_rows(dp_x), fold_rows(dp_x), y1)
+
+    order = ((0, 0), (1, 0), (0, 1), (1, 1))
+    z_copies = {}
+    for index, part in order:
+        x_copies[index, part].wait_recv()
+        area = pl.ds(part * half, half)
+        met = total[2 * index, area] + x_recv[index, part].astype(jnp.float32)
+        total[2 * index, area] = met
+        z_send[index, part] = met.astype(jnp.bfloat16)
+        z_copies[index, part] = remote(z_send.at[index, part], z_recv.at[1 - index, part], z1)
+    pairs, onward = {}, {}
+
+    def area_of(core_side, part):
+        return pl.ds(core_side * rows + part * half, half)
+
+    def to_partner(unit, part):
+        pairs[unit, part] = remote(
+            encoded.at[unit, area_of(0, part)], encoded.at[unit, area_of(1, part)], pc
+        )
+
+    for index, part in order:
+        z_copies[1 - index, part].wait_recv()
+        area = pl.ds(part * half, half)
+        encoded[index, area_of(0, part)] = (
+            pixels[2 * index, area].astype(jnp.float32)
+            + total[2 * index, area]
+            + z_recv[index, part].astype(jnp.float32)
+        ).astype(jnp.bfloat16)
+        if index == 0:
+            onward[2, part] = remote(
+                encoded.at[0, area_of(0, part)], encoded.at[2, area_of(0, part)], z2
+            )
+        to_partner(index, part)
+
+    fold_local.wait()
+    fold_y.wait_recv()
+    fold_d.wait_recv()
+    scale = 1.0 / HEAD_DIM**0.5
+    limit = tile_count[0] * TILE_TOK
+
+    def attend(unit, unit_spot):
+        count = 2 * rows
+        kv_block = jnp.dot(encoded[unit], folded[...], preferred_element_type=jnp.float32)
+        key = kv_block[:, :HEAD_DIM]
+        key_scale = lax.rsqrt(jnp.mean(key * key, axis=-1, keepdims=True) + 1e-06)
+        keys[...] = (key * key_scale).astype(jnp.bfloat16)
+        values[...] = kv_block[:, HEAD_DIM:].astype(jnp.bfloat16)
+        place = lax.broadcasted_iota(jnp.int32, (1, count), 1)
+        own_base = (unit_spot * CORES + core) * rows
+        other_base = (unit_spot * CORES + 1 - core) * rows - rows
+        token = place + jnp.where(place < rows, own_base, other_base)
+        valid = token < limit
+
+        def one(group, carry):
+            scores = (
+                lax.dot_general(
+                    queries[group],
+                    keys[...],
+                    (((1,), (1,)), ((), ())),
+                    preferred_element_type=jnp.float32,
+                )
+                * scale
+            )
+            scores = jnp.where(valid, scores, -1e30)
+            top = jnp.max(scores, axis=-1, keepdims=True)
+            if unit > 0:
+                before = tops[group][:, :1]
+                top = jnp.maximum(before, top)
+                shrink = jnp.exp(before - top)
+            weights = jnp.exp(scores - top)
+            weight_sum = jnp.sum(weights, axis=-1, keepdims=True)
+            blend = jnp.dot(
+                weights.astype(jnp.bfloat16), values[...], preferred_element_type=jnp.float32
+            )
+            if unit > 0:
+                weight_sum += shrink * sums[group][:, :1]
+                blend += shrink * mixed[group]
+            tops[group] = jnp.broadcast_to(top, tops.shape[1:])
+            sums[group] = jnp.broadcast_to(weight_sum, sums.shape[1:])
+            mixed[group] = blend
+            return carry
+
+        lax.fori_loop(0, queries.shape[0], one, 0)
+
+    for part in range(2):
+        pairs[0, part].wait_recv()
+    attend(0, spot)
+
+    def pass_on(part):
+        onward[2, part].wait_recv()
+        onward[3, part] = remote(
+            encoded.at[2, area_of(0, part)], encoded.at[3, area_of(0, part)], z1
+        )
+        to_partner(2, part)
+
+    pass_on(0)
+    for part in range(2):
+        pairs[1, part].wait_recv()
+    attend(1, spot_1)
+    pass_on(1)
+    for part in range(2):
+        pairs[2, part].wait_recv()
+    attend(2, spot_2)
+    for part in range(2):
+        onward[3, part].wait_recv()
+        to_partner(3, part)
+    for part in range(2):
+        pairs[3, part].wait_recv()
+    attend(3, spot_3)
+
+    text_at = lax.broadcasted_iota(jnp.int32, (text_rows, 1), 0)
+    row_mask = (text_at >= text_start[0]).astype(jnp.float32)
+    for head in range(head_count):
+        area = pl.ds(head % 2 * text_rows, text_rows)
+        heads[:, head * HEAD_DIM : (head + 1) * HEAD_DIM] = (
+            mixed[head // 2, area] / sums[head // 2, area][:, :1] * row_mask
+        ).astype(jnp.bfloat16)
+
+    steps = o_part.shape[0]
+    base = len(started)
+
+    def o_remote(kind, step, source, target, peer):
+        return pltpu.make_async_remote_copy(
+            src_ref=source,
+            dst_ref=target,
+            send_sem=sends.at[base + kind * steps + step],
+            recv_sem=recvs.at[base + kind * steps + step],
+            device_id=peer,
+            device_id_type=MESH,
+        )
+
+    def o_first(step):
+        return o_remote(0, step, o_part.at[step, :, :, 1 - core], o_0.at[step], pc)
+
+    def o_second(step):
+        return o_remote(1, step, o_1.at[step, :, 1 - low], o_2.at[step], z1)
+
+    def o_third(step):
+        return o_remote(2, step, o_3.at[step, 1 - high], o_4.at[step], z2)
+
+    def meet_first(step):
+        o_first(step).wait_recv()
+        o_1[step] = (
+            o_part[step, :, :, core].astype(jnp.float32) + o_0[step].astype(jnp.float32)
+        ).astype(jnp.bfloat16)
+        o_second(step).start()
+
+    def meet_second(step):
+        o_second(step).wait_recv()
+        o_3[step] = (
+            o_1[step, :, low].astype(jnp.float32) + o_2[step].astype(jnp.float32)
+        ).astype(jnp.bfloat16)
+        o_third(step).start()
+
+    def o_step(step, carry):
+        o_copy(step).wait()
+        slot = lax.rem(step, stages)
+        result = jnp.dot(heads[...], staged[slot], preferred_element_type=jnp.float32)
+        o_part[step] = result.reshape(o_part.shape[1:]).astype(jnp.bfloat16)
+        o_first(step).start()
+
+        @pl.when(step + stages < steps)
+        def _():
+            o_copy(step + stages).start()
+
+        @pl.when(step > 1)
+        def _():
+            meet_first(step - 2)
+
+        return carry
+
+    lax.fori_loop(0, steps, o_step, 0)
+    meet_first(steps - 2)
+    meet_first(steps - 1)
+
+    def second(step, carry):
+        meet_second(step)
+        return carry
+
+    lax.fori_loop(0, steps, second, 0)
+
+    def third(step, carry):
+        o_third(step).wait_recv()
+        out[:, pl.ds(pl.multiple_of(step * depth, depth), depth)] = (
+            o_3[step, high].astype(jnp.float32) + o_4[step].astype(jnp.float32)
+        ).astype(jnp.bfloat16)
+        return carry
+
+    lax.fori_loop(0, steps, third, 0)
+    for copy in started:
+        copy.wait_send()
+
+    def drain(step, carry):
+        o_first(step).wait_send()
+        o_second(step).wait_send()
+        o_third(step).wait_send()
+        return carry
+
+    lax.fori_loop(0, steps, drain, 0)
+
+
+def fused(image, gain, fc1, fc2, projector, kv, text, q_weight, o_weight, tile_count, text_start):
+    rows, width = image.shape
+    hidden = fc1.shape[0]
+    part_rows = projector.shape[0] // lax.axis_size("dp")
+    depth = projector.shape[1]
+    columns = kv.shape[1] // lax.axis_size("mp")
+    text_rows = text.shape[0]
+    query_columns = q_weight.shape[1]
+    pairs = query_columns // HEAD_DIM // 2
+    half = rows // 2
+    token_rows = text_rows // lax.axis_size("mp")
+    steps = o_weight.shape[1] // depth
+    low, wide = jnp.bfloat16, jnp.float32
+    copies = 64 + 3 * steps
+    scratch = [
+        ((4, 2 * hidden, width), low),
+        ((4, 2 * hidden, width), low),
+        ((4, rows, width), low),
+        ((4, rows, width), low),
+        ((4, rows, width), wide),
+        ((2, 2, half, width), low),
+        ((2, 2, half, width), low),
+        ((2, 2, half, width), low),
+        ((2, 2, half, width), low),
+        ((4, 2 * rows, width), low),
+        ((part_rows, depth), low),
+        ((4, CORES, part_rows, columns), low),
+        ((4, part_rows, columns), low),
+        ((2, 2, part_rows, columns), low),
+        ((2, part_rows, columns), low),
+        ((2, part_rows, columns), low),
+        ((part_rows, columns), low),
+        ((part_rows, columns), low),
+        ((width, columns), low),
+        (text.shape, low),
+        ((4, depth, depth), low),
+        ((text_rows, query_columns), wide),
+        ((pairs, 2 * text_rows, HEAD_DIM), low),
+        ((2 * rows, HEAD_DIM), low),
+        ((2 * rows, HEAD_DIM), low),
+        ((pairs, 2 * text_rows, HEAD_DIM), wide),
+        ((pairs, 2 * text_rows, HEAD_DIM), wide),
+        ((pairs, 2 * text_rows, HEAD_DIM), wide),
+        ((text_rows, query_columns), low),
+        ((steps, 2, 2, CORES, token_rows, depth), low),
+        ((steps, 2, 2, token_rows, depth), low),
+        ((steps, 2, 2, token_rows, depth), low),
+        ((steps, 2, token_rows, depth), low),
+        ((steps, 2, token_rows, depth), low),
+        ((steps, token_rows, depth), low),
+    ]
+    vmem, anywhere = pl.BlockSpec(memory_space=pltpu.VMEM), pl.BlockSpec(memory_space=pl.ANY)
+    smem = pl.BlockSpec(memory_space=pltpu.SMEM)
+    return pl.pallas_call(
+        fused_kernel,
+        out_shape=jax.ShapeDtypeStruct((token_rows, o_weight.shape[1]), jnp.bfloat16),
+        in_specs=[anywhere, vmem] + [anywhere] * 7 + [smem, smem],
+        out_specs=vmem,
+        scratch_shapes=[pltpu.VMEM(shape, kind) for shape, kind in scratch]
+        + [
+            pltpu.SemaphoreType.DMA((16,)),
+            pltpu.SemaphoreType.DMA((4,)),
+            pltpu.SemaphoreType.DMA((copies,)),
+            pltpu.SemaphoreType.DMA((copies,)),
+        ],
+        compiler_params=pltpu.CompilerParams(
+            collective_id=7, has_side_effects=True, vmem_limit_bytes=67043328
+        ),
+        name="fused",
+    )(image, gain, fc1, fc2, projector, kv, text, q_weight, o_weight, tile_count, text_start)
+
+
+def paired_local(
+    image,
+    ln_gain,
+    fc1_weight,
+    fc2_weight,
+    projector_weight,
+    kv_weight,
+    text,
+    q_weight,
+    o_weight,
+    tile_count,
+    text_start,
+):
+    return fused(
+        image[0],
+        ln_gain[None],
+        fc1_weight.T,
+        fc2_weight,
+        projector_weight,
+        kv_weight.reshape(kv_weight.shape[0], -1),
+        text[0],
+        q_weight,
+        o_weight,
+        tile_count,
+        text_start,
+    )[None]
+
+
+def choose(*arrays):
+    groups, members = lax.axis_size("dp"), lax.axis_size("mp")
+    pairs_of_pairs = groups == members // CORES == 2 * 2
+    if pairs_of_pairs and arrays[5].shape[1] == members:
+        return paired_local(*arrays)
+    return local(*arrays)
+
+
 def solution(mesh):
     return jax.shard_map(
-        local,
+        choose,
         mesh=mesh,
         in_specs=(
             P("dp", "mp", None),

time: 262 us -> 186 us (0.71)
  matrix products: 60 us -> 0 us
  other arithmetic: 15.5 us -> 0 us
    dot_general x6 -> x0, matrix products: 52.3 us -> none  [the longest x1 21.3 us: local(): jnp.dot(hidden, down, preferred_element_type=jnp.float32)]
    reduce_sum x6 -> x0, other arithmetic: 9.49 us -> none  [the longest x1 2.24 us: local(): jnp.sum(terms.astype(jnp.float32), axis=0)]
    sub x1 -> x0, matrix products: 7.71 us -> none  [attend_block(): weights = jnp.exp(scores - top)]
    convert_element_type x5 -> x0, other arithmetic: 5.98 us -> none  [the longest x1 2.77 us: local(): (mine.astype(jnp.float32) + theirs.astype(jnp.float32)).astype(jnp.bfloat16)]
    pallas_call x5 -> x1, Pallas kernels: 173 us -> 173 us  [fused(): pl.pallas_call(fused_kernel, out_shape=jax.ShapeDtypeStruct((token_rows,...]
where the time goes in v1:
time: 186 us; the launch traced here: 185 us
  Pallas kernels  173 us (93%)
  local copies, waits for them, and re-layouts  10.8 us (6%)
    pallas_call x1, Pallas kernels, fused(): pl.pallas_call(fused_kernel, out_shape=jax.ShapeDtypeStruct((token_rows,...  173 us
    reshape x1, local copies, waits for them, and re-layouts, paired_local(): kv_weight.reshape(kv_weight.shape[0], -1)  7.79 us

profile of v1, /device:TPU:0, one launch (start us, length us, event | category | flops | bytes accessed | tf_op | source)
XLA Modules:
  0.0 185.2 jit_solution(3872270939845959346)
XLA Ops:
  1.3 1.3 broadcast_in_dim.6.gain
  2.6 7.8 %reshape.3.kv = bf16[1024,2048]{1,0:T(8,128)(2,1)} reshape(bf16[1024,8,2,128]{3,2,1,0:T(2,128)(2,1)} %param.16) | data formatting | bytes 8388608 | tf_op jit(solution)/shard_map/reshape | solution.py:926
  10.4 173.1 %fused.1 = bf16[16,8192]{1,0:T(8,128)(2,1)} custom-call(bf16[256,1280]{1,0:T(8,128)(2,1)} %bitcast.6, f32[1,1280]{1,0:T(1,128)} %broadcast_in_dim.6.gain, bf16[160,1280]{1,0:T(8,128)(2,1)} %bitcast.7, bf16[160,1280]{1,0:T(8,128)(2,1)} %fc2.1, bf16[1280,1024]{1,0:T(8,128)(2,1)} %projector.1, bf16[1024,2048]{1,0:T(8,128)(2,1)} %reshape.3.kv, ...), custom_call_target="tpu_custom_call" | custom-call | tf_op jit(solution)/shard_map/fused/pallas_call | solution.py:888
  183.5 1.7 copy.15

commit v2 on v1

--- a/solution.py
+++ b/solution.py
@@ -350,6 +350,8 @@
     z_recv,
     encoded,
     rows_part,
+    kv_raw,
+    kv_flat,
     fold_part,
     fold_0,
     fold_1,
@@ -411,16 +413,8 @@
     stages = staged.shape[0]
     half = rows // 2
 
-    kv_parts = kv.shape[1] // depth
-    kv_copies = [
-        local(kv.at[:, pl.ds(i * depth, depth)], staged.at[i]) for i in range(kv_parts)
-    ]
-    part_copy = local(
-        projector.at[pl.ds(pl.multiple_of(dp * part_rows, part_rows), part_rows)], rows_part
-    )
-
     def q_copy(step):
-        slot = lax.rem(step + kv_parts, stages)
+        slot = lax.rem(step, stages)
         return pltpu.make_async_copy(
             q_weight.at[pl.ds(pl.multiple_of(step * depth, depth), depth)],
             staged.at[slot],
@@ -435,12 +429,16 @@
             stage_sem.at[slot],
         )
 
-    text_copy = local(text, words)
-    for step in range(stages - kv_parts):
-        q_copy(step).start()
     image_copy = local(image, pixels.at[0])
     up_copy = local(fc1, up.at[0, pl.ds(0, hidden)])
     down_copy = local(fc2, down.at[0, pl.ds(0, hidden)])
+    text_copy = local(text, words)
+    for step in range(stages):
+        q_copy(step).start()
+    kv_copy = local(kv, kv_raw)
+    part_copy = local(
+        projector.at[pl.ds(pl.multiple_of(dp * part_rows, part_rows), part_rows)], rows_part
+    )
 
     pl.semaphore_wait(barrier, 5)
 
@@ -461,33 +459,16 @@
         return copy
 
     mine, theirs = pl.ds(0, hidden), pl.ds(hidden, hidden)
-    image_z = remote(image, pixels.at[2], z1)
+    halves = [pl.ds(part * half, half) for part in range(2)]
+    bits = [pl.ds(part * (hidden // 2), hidden // 2) for part in range(2)]
+    image_z = [remote(image.at[area], pixels.at[2, area], z1) for area in halves]
     image_x = remote(image, pixels.at[1], x1)
-    up_z = remote(fc1, up.at[2, mine], z2)
-    down_z = remote(fc2, down.at[2, mine], z2)
+    up_z = [remote(fc1.at[area], up.at[2, area], z2) for area in bits]
+    down_z = [remote(fc2.at[area], down.at[2, area], z2) for area in bits]
     up_y = remote(fc1, up.at[1, mine], y1)
     down_y = remote(fc2, down.at[1, mine], y1)
-    up_p = [remote(fc1, up.at[0, theirs], pc)]
-    down_p = [remote(fc2, down.at[0, theirs], pc)]
-
-    for copy in kv_copies:
-        copy.wait()
-    part_copy.wait()
-    columns = fold_part.shape[-1]
-    per_stage = depth // columns
-
-    def fold_step(head, carry):
-        start = pl.multiple_of(lax.rem(head, per_stage) * columns, columns)
-        block = staged[lax.div(head, per_stage), :, pl.ds(start, columns)]
-        fold_part[lax.div(head, CORES), lax.rem(head, CORES)] = jnp.dot(
-            rows_part[...], block, preferred_element_type=jnp.float32
-        ).astype(jnp.bfloat16)
-        return carry
-
-    lax.fori_loop(0, fold_part.shape[0] * CORES, fold_step, 0)
-    fold_p = remote(fold_part.at[:, 1 - core], fold_0, pc)
-    for step in range(stages - kv_parts, stages):
-        q_copy(step).start()
+    up_p = {0: remote(fc1, up.at[0, theirs], pc)}
+    down_p = {0: remote(fc2, down.at[0, theirs], pc)}
 
     text_copy.wait()
     q_steps = q_weight.shape[0] // depth
@@ -495,10 +476,9 @@
 
     def q_step(step, carry):
         q_copy(step).wait()
-        slot = lax.rem(step + kv_parts, stages)
         q_total[...] += jnp.dot(
             words[:, pl.ds(pl.multiple_of(step * depth, depth), depth)],
-            staged[slot],
+            staged[lax.rem(step, stages)],
             preferred_element_type=jnp.float32,
         )
 
@@ -515,8 +495,6 @@
         queries[head // 2, pl.ds(head % 2 * text_rows, text_rows)] = q_total[
             :, head * HEAD_DIM : (head + 1) * HEAD_DIM
         ].astype(jnp.bfloat16)
-    for step in range(stages):
-        o_copy(step).start()
 
     strip = 32
 
@@ -556,9 +534,54 @@
     up_p[0].wait_recv()
     down_p[0].wait_recv()
     mlp(0, True, 1, 0)
-    image_z.wait_recv()
-    image_d = remote(pixels.at[2], pixels.at[3], x1)
+    kv_copy.wait()
+    flat = 16
+
+    def flatten(step, carry):
+        area = pl.ds(pl.multiple_of(step * flat, flat), flat)
+        kv_flat[area] = kv_raw[area].reshape(flat, kv_flat.shape[1])
+        return carry
+
+    lax.fori_loop(0, kv_flat.shape[0] // flat, flatten, 0)
+    part_copy.wait()
+    columns = fold_part.shape[-1]
+
+    def fold_step(head, carry):
+        block = kv_flat[:, pl.ds(pl.multiple_of(head * columns, columns), columns)]
+        fold_part[lax.div(head, CORES), lax.rem(head, CORES)] = jnp.dot(
+            rows_part[...], block, preferred_element_type=jnp.float32
+        ).astype(jnp.bfloat16)
+        return carry
+
+    lax.fori_loop(0, fold_part.shape[0] * CORES, fold_step, 0)
+    fold_p = remote(fold_part.at[:, 1 - core], fold_0, pc)
+    for step in range(stages):
+        o_copy(step).start()
+    image_x.wait_recv()
+    normalise(1)
+    mlp(0, True, 1, 1)
+    up_y.wait_recv()
+    up_p[1] = remote(up.at[1, mine], up.at[1, theirs], pc)
+    down_y.wait_recv()
+    down_p[1] = remote(down.at[1, mine], down.at[1, theirs], pc)
+    up_d, down_d = [], []
+    for part, copy in enumerate(up_z):
+        copy.wait_recv()
+        up_d.append(remote(up.at[2, bits[part]], up.at[3, bits[part]], y1))
+    up_p[2] = remote(up.at[2, mine], up.at[2, theirs], pc)
+    image_d = []
+    image_z[0].wait_recv()
+    image_d.append(remote(pixels.at[2, halves[0]], pixels.at[3, halves[0]], x1))
+    up_p[1].wait_recv()
+    down_p[1].wait_recv()
+    mlp(1, False, 2, 0)
+    image_z[1].wait_recv()
+    image_d.append(remote(pixels.at[2, halves[1]], pixels.at[3, halves[1]], x1))
     normalise(2)
+    for part, copy in enumerate(down_z):
+        copy.wait_recv()
+        down_d.append(remote(down.at[2, bits[part]], down.at[3, bits[part]], y1))
+    down_p[2] = remote(down.at[2, mine], down.at[2, theirs], pc)
     fold_p.wait_recv()
     spots = fold_0.shape[0]
 
@@ -569,51 +592,24 @@
         return carry
 
     lax.fori_loop(0, spots, fold_pair, 0)
-    image_x.wait_recv()
-    normalise(1)
-    mlp(0, True, 2, 1)
-
-    up_z.wait_recv()
-    up_d = remote(up.at[2, mine], up.at[3, mine], y1)
-    up_p.append(remote(up.at[2, mine], up.at[2, theirs], pc))
-    up_y.wait_recv()
-    up_p.append(remote(up.at[1, mine], up.at[1, theirs], pc))
-    down_y.wait_recv()
-    down_p.append(remote(down.at[1, mine], down.at[1, theirs], pc))
-    image_d.wait_recv()
+    fold_z = remote(fold_1.at[:, 1 - low], fold_2, z1)
+    mlp(0, True, 1, 2)
+    mlp(1, False, 1, 2)
+    up_p[2].wait_recv()
+    down_p[2].wait_recv()
+    mlp(2, False, 3, 0)
+    for copy in image_d:
+        copy.wait_recv()
     normalise(3)
+    for copy in up_d:
+        copy.wait_recv()
+    up_p[3] = remote(up.at[3, mine], up.at[3, theirs], pc)
     mlp(0, True, 1, 3)
-    down_z.wait_recv()
-    down_d = remote(down.at[2, mine], down.at[3, mine], y1)
-    down_p.append(remote(down.at[2, mine], down.at[2, theirs], pc))
-    fold_z = remote(fold_1.at[:, 1 - low], fold_2, z1)
-    up_p[2].wait_recv()
-    down_p[1].wait_recv()
-    mlp(1, False, 4, 0)
-    up_p[1].wait_recv()
-    down_p[2].wait_recv()
-    mlp(2, False, 4, 0)
-    fold_z.wait_recv()
-    for index in range(2):
-        fold_3[index] = (
-            fold_1[index, low].astype(jnp.float32) + fold_2[index].astype(jnp.float32)
-        ).astype(jnp.bfloat16)
-    fold_zz = remote(fold_3.at[1 - high], fold_4, z2)
-    up_d.wait_recv()
-    up_p.append(remote(up.at[3, mine], up.at[3, theirs], pc))
-    fold_zz.wait_recv()
-    fold_own[...] = (
-        fold_3[high].astype(jnp.float32) + fold_4[...].astype(jnp.float32)
-    ).astype(jnp.bfloat16)
-
-    def fold_rows(owner):
-        return folded.at[pl.ds(pl.multiple_of(owner * part_rows, part_rows), part_rows)]
-
-    fold_local = local(fold_own, fold_rows(dp))
-    fold_x = remote(fold_own, fold_rows(dp), x1)
-    fold_y = remote(fold_own, fold_rows(dp), y1)
-    down_d.wait_recv()
-    down_p.append(remote(down.at[3, mine], down.at[3, theirs], pc))
+    mlp(1, False, 1, 3)
+    mlp(2, False, 1, 3)
+    for copy in down_d:
+        copy.wait_recv()
+    down_p[3] = remote(down.at[3, mine], down.at[3, theirs], pc)
     up_p[3].wait_recv()
     down_p[3].wait_recv()
 
@@ -629,18 +625,33 @@
     x_copies[0, 1] = to_x(1, 1)
     x_copies[1, 1] = to_x(3, 1)
     mlp(3, False, 2, 0, 2)
-    fold_x.wait_recv()
-    fold_d = remote(fold_rows(dp_x), fold_rows(dp_x), y1)
+    fold_z.wait_recv()
+    for index in range(2):
+        fold_3[index] = (
+            fold_1[index, low].astype(jnp.float32) + fold_2[index].astype(jnp.float32)
+        ).astype(jnp.bfloat16)
+    fold_zz = remote(fold_3.at[1 - high], fold_4, z2)
+
+    def fold_rows(owner):
+        return folded.at[pl.ds(pl.multiple_of(owner * part_rows, part_rows), part_rows)]
 
     order = ((0, 0), (1, 0), (0, 1), (1, 1))
     z_copies = {}
-    for index, part in order:
+    for number, (index, part) in enumerate(order):
         x_copies[index, part].wait_recv()
         area = pl.ds(part * half, half)
         met = total[2 * index, area] + x_recv[index, part].astype(jnp.float32)
         total[2 * index, area] = met
         z_send[index, part] = met.astype(jnp.bfloat16)
         z_copies[index, part] = remote(z_send.at[index, part], z_recv.at[1 - index, part], z1)
+        if number == 0:
+            fold_zz.wait_recv()
+            fold_own[...] = (
+                fold_3[high].astype(jnp.float32) + fold_4[...].astype(jnp.float32)
+            ).astype(jnp.bfloat16)
+            fold_local = local(fold_own, fold_rows(dp))
+            fold_y = remote(fold_own, fold_rows(dp), y1)
+            fold_x = remote(fold_own, fold_rows(dp), x1)
     pairs, onward = {}, {}
 
     def area_of(core_side, part):
@@ -666,6 +677,8 @@
         to_partner(index, part)
 
     fold_local.wait()
+    fold_x.wait_recv()
+    fold_d = remote(fold_rows(dp_x), fold_rows(dp_x), y1)
     fold_y.wait_recv()
     fold_d.wait_recv()
     scale = 1.0 / HEAD_DIM**0.5
@@ -837,7 +850,8 @@
     hidden = fc1.shape[0]
     part_rows = projector.shape[0] // lax.axis_size("dp")
     depth = projector.shape[1]
-    columns = kv.shape[1] // lax.axis_size("mp")
+    kv_columns = kv.shape[1] * kv.shape[2] * kv.shape[3]
+    columns = kv_columns // lax.axis_size("mp")
     text_rows = text.shape[0]
     query_columns = q_weight.shape[1]
     pairs = query_columns // HEAD_DIM // 2
@@ -858,6 +872,8 @@
         ((2, 2, half, width), low),
         ((4, 2 * rows, width), low),
         ((part_rows, depth), low),
+        (kv.shape, low),
+        ((kv.shape[0], kv_columns), low),
         ((4, CORES, part_rows, columns), low),
         ((4, part_rows, columns), low),
         ((2, 2, part_rows, columns), low),
@@ -919,11 +935,11 @@
 ):
     return fused(
         image[0],
-        ln_gain[None],
+        ln_gain,
         fc1_weight.T,
         fc2_weight,
         projector_weight,
-        kv_weight.reshape(kv_weight.shape[0], -1),
+        kv_weight,
         text[0],
         q_weight,
         o_weight,

time: 186 us -> 158 us (0.85)
  Pallas kernels: 173 us -> 155 us
  local copies, waits for them, and re-layouts: 10.8 us -> 1.67 us
    pallas_call x1, Pallas kernels: 173 us -> 155 us  [fused(): pl.pallas_call(fused_kernel, out_shape=jax.ShapeDtypeStruct((token_rows,...]
    reshape x1 -> x0, local copies, waits for them, and re-layouts: 7.79 us -> none  [paired_local(): kv_weight.reshape(kv_weight.shape[0], -1)]
where the time goes in v2:
time: 158 us
  Pallas kernels  155 us (98%)
  local copies, waits for them, and re-layouts  1.67 us (1%)
    pallas_call x1, Pallas kernels, fused(): pl.pallas_call(fused_kernel, out_shape=jax.ShapeDtypeStruct((token_rows,...  155 us

profile of v2, /device:TPU:0, one launch (start us, length us, event | category | flops | bytes accessed | tf_op | source)
XLA Modules:
  0.0 157.5 jit_solution(3282631074538501137)
XLA Ops:
  1.3 154.5 %fused.1 = bf16[16,8192]{1,0:T(8,128)(2,1)} custom-call(bf16[256,1280]{1,0:T(8,128)(2,1)} %bitcast.6, f32[1280]{0:T(1024)} %gain.1, bf16[160,1280]{1,0:T(8,128)(2,1)} %bitcast.7, bf16[160,1280]{1,0:T(8,128)(2,1)} %fc2.1, bf16[1280,1024]{1,0:T(8,128)(2,1)} %projector.1, bf16[1024,8,2,128]{3,2,1,0:T(2,128)(2,1)} %kv.1, bf16[128,8192]{1,0:T(8,128)(2,1)} %bitcast.4, ...), custom_call_target="tpu_custom_call" | custom-call | tf_op jit(solution)/shard_map/fused/pallas_call | solution.py:904
  155.8 1.7 %copy.15 = bf16[1,16,8192]{2,1,0:T(8,128)(2,1)} copy(bf16[1,16,8192]{2,1,0:T(8,128)(2,1)} %bitcast.5) | data formatting | bytes 524288

commit v3 on v2

--- a/solution.py
+++ b/solution.py
@@ -344,6 +344,7 @@
     pixels,
     normed,
     total,
+    held,
     x_send,
     x_recv,
     z_send,
@@ -411,7 +412,6 @@
     part_rows = rows_part.shape[0]
     depth = staged.shape[1]
     stages = staged.shape[0]
-    half = rows // 2
 
     def q_copy(step):
         slot = lax.rem(step, stages)
@@ -459,9 +459,12 @@
         return copy
 
     mine, theirs = pl.ds(0, hidden), pl.ds(hidden, hidden)
-    halves = [pl.ds(part * half, half) for part in range(2)]
-    bits = [pl.ds(part * (hidden // 2), hidden // 2) for part in range(2)]
-    image_z = [remote(image.at[area], pixels.at[2, area], z1) for area in halves]
+    parts = x_send.shape[1]
+    slim = rows // parts
+    slices = [pl.ds(part * slim, slim) for part in range(parts)]
+    piece = 32
+    bits = [pl.ds(begin, piece) for begin in range(0, hidden, piece)]
+    image_z = [remote(image.at[area], pixels.at[2, area], z1) for area in slices]
     image_x = remote(image, pixels.at[1], x1)
     up_z = [remote(fc1.at[area], up.at[2, area], z2) for area in bits]
     down_z = [remote(fc2.at[area], down.at[2, area], z2) for area in bits]
@@ -523,6 +526,29 @@
                     total[row, :, area] = term
                 else:
                     total[row, :, area] += term
+            return carry
+
+        lax.fori_loop(0, last, one, 0)
+
+    def widen(block, last, base, stride=1):
+        def one(step, carry):
+            row = base + step * stride
+            inner = lax.dot_general(
+                normed[row], up[block], (((1,), (1,)), ((), ())), preferred_element_type=jnp.float32
+            )
+            held[block - 2, row] = erf_gelu(inner).astype(jnp.bfloat16)
+            return carry
+
+        lax.fori_loop(0, last, one, 0)
+
+    def narrow(block, last, base, stride=1):
+        def one(step, carry):
+            row = base + step * stride
+            for begin in range(0, total.shape[-1], tile):
+                area = pl.ds(begin, tile)
+                total[row, :, area] += jnp.dot(
+                    held[block - 2, row], down[block, :, area], preferred_element_type=jnp.float32
+                )
             return carry
 
         lax.fori_loop(0, last, one, 0)
@@ -570,17 +596,31 @@
         up_d.append(remote(up.at[2, bits[part]], up.at[3, bits[part]], y1))
     up_p[2] = remote(up.at[2, mine], up.at[2, theirs], pc)
     image_d = []
-    image_z[0].wait_recv()
-    image_d.append(remote(pixels.at[2, halves[0]], pixels.at[3, halves[0]], x1))
+
+    def image_on(part):
+        image_z[part].wait_recv()
+        image_d.append(remote(pixels.at[2, slices[part]], pixels.at[3, slices[part]], x1))
+
+    def down_on(part):
+        down_z[part].wait_recv()
+        down_d.append(remote(down.at[2, bits[part]], down.at[3, bits[part]], y1))
+
+    for part in range(parts - 1):
+        image_on(part)
     up_p[1].wait_recv()
     down_p[1].wait_recv()
     mlp(1, False, 2, 0)
-    image_z[1].wait_recv()
-    image_d.append(remote(pixels.at[2, halves[1]], pixels.at[3, halves[1]], x1))
+    down_on(0)
+    up_p[2].wait_recv()
+    widen(2, 2, 0)
+    image_on(parts - 1)
+    down_on(1)
     normalise(2)
-    for part, copy in enumerate(down_z):
-        copy.wait_recv()
-        down_d.append(remote(down.at[2, bits[part]], down.at[3, bits[part]], y1))
+    down_on(2)
+    mlp(0, True, 1, 2)
+    mlp(1, False, 1, 2)
+    for part in range(3, len(bits)):
+        down_on(part)
     down_p[2] = remote(down.at[2, mine], down.at[2, theirs], pc)
     fold_p.wait_recv()
     spots = fold_0.shape[0]
@@ -593,38 +633,47 @@
 
     lax.fori_loop(0, spots, fold_pair, 0)
     fold_z = remote(fold_1.at[:, 1 - low], fold_2, z1)
-    mlp(0, True, 1, 2)
-    mlp(1, False, 1, 2)
-    up_p[2].wait_recv()
+    for copy in up_d:
+        copy.wait_recv()
+    up_p[3] = remote(up.at[3, mine], up.at[3, theirs], pc)
+    up_p[3].wait_recv()
+    widen(3, 1, 1)
     down_p[2].wait_recv()
-    mlp(2, False, 3, 0)
+    narrow(2, 1, 1)
     for copy in image_d:
         copy.wait_recv()
     normalise(3)
-    for copy in up_d:
-        copy.wait_recv()
-    up_p[3] = remote(up.at[3, mine], up.at[3, theirs], pc)
     mlp(0, True, 1, 3)
     mlp(1, False, 1, 3)
-    mlp(2, False, 1, 3)
-    for copy in down_d:
+    widen(2, 1, 3)
+    spread = []
+    for part, copy in enumerate(down_d):
         copy.wait_recv()
-    down_p[3] = remote(down.at[3, mine], down.at[3, theirs], pc)
-    up_p[3].wait_recv()
-    down_p[3].wait_recv()
+        mirror = pl.ds(hidden + part * piece, piece)
+        spread.append(remote(down.at[3, bits[part]], down.at[3, mirror], pc))
+    for copy in spread:
+        copy.wait_recv()
 
     def to_x(row, part):
         index = row // 2
-        x_send[index, part] = total[row, pl.ds(part * half, half)].astype(jnp.bfloat16)
+        x_send[index, part] = total[row, slices[part]].astype(jnp.bfloat16)
         return remote(x_send.at[index, part], x_recv.at[index, part], x1)
 
-    mlp(3, False, 1, 1)
-    x_copies = {(0, 0): to_x(1, 0)}
-    mlp(3, False, 1, 3)
-    x_copies[1, 0] = to_x(3, 0)
-    x_copies[0, 1] = to_x(1, 1)
-    x_copies[1, 1] = to_x(3, 1)
-    mlp(3, False, 2, 0, 2)
+    narrow(3, 1, 1)
+    x_copies = {(0, 0): to_x(1, 0), (0, 1): to_x(1, 1)}
+    widen(3, 1, 3)
+    narrow(2, 1, 3)
+    narrow(3, 1, 3)
+    order = [(0, 0), (0, 1)]
+    for part in range(2, parts):
+        order += [(1, part - 2), (0, part)]
+    order += [(1, part) for part in range(parts - 2, parts)]
+    for index, part in order[2:]:
+        x_copies[index, part] = to_x(2 * index + 1, part)
+    widen(2, 1, 2)
+    widen(3, 2, 0, 2)
+    narrow(2, 2, 0, 2)
+    narrow(3, 2, 0, 2)
     fold_z.wait_recv()
     for index in range(2):
         fold_3[index] = (
@@ -635,36 +684,19 @@
     def fold_rows(owner):
         return folded.at[pl.ds(pl.multiple_of(owner * part_rows, part_rows), part_rows)]
 
-    order = ((0, 0), (1, 0), (0, 1), (1, 1))
-    z_copies = {}
-    for number, (index, part) in enumerate(order):
-        x_copies[index, part].wait_recv()
-        area = pl.ds(part * half, half)
-        met = total[2 * index, area] + x_recv[index, part].astype(jnp.float32)
-        total[2 * index, area] = met
-        z_send[index, part] = met.astype(jnp.bfloat16)
-        z_copies[index, part] = remote(z_send.at[index, part], z_recv.at[1 - index, part], z1)
-        if number == 0:
-            fold_zz.wait_recv()
-            fold_own[...] = (
-                fold_3[high].astype(jnp.float32) + fold_4[...].astype(jnp.float32)
-            ).astype(jnp.bfloat16)
-            fold_local = local(fold_own, fold_rows(dp))
-            fold_y = remote(fold_own, fold_rows(dp), y1)
-            fold_x = remote(fold_own, fold_rows(dp), x1)
-    pairs, onward = {}, {}
+    z_copies, pairs, onward = {}, {}, {}
 
     def area_of(core_side, part):
-        return pl.ds(core_side * rows + part * half, half)
+        return pl.ds(core_side * rows + part * slim, slim)
 
     def to_partner(unit, part):
         pairs[unit, part] = remote(
             encoded.at[unit, area_of(0, part)], encoded.at[unit, area_of(1, part)], pc
         )
 
-    for index, part in order:
+    def encode(index, part):
         z_copies[1 - index, part].wait_recv()
-        area = pl.ds(part * half, half)
+        area = slices[part]
         encoded[index, area_of(0, part)] = (
             pixels[2 * index, area].astype(jnp.float32)
             + total[2 * index, area]
@@ -676,9 +708,48 @@
             )
         to_partner(index, part)
 
-    fold_local.wait()
+    ready = [(index, part) for part in range(parts) for index in range(2)]
+    count = 0
+    for number, (index, part) in enumerate(order):
+        x_copies[index, part].wait_recv()
+        area = slices[part]
+        met = total[2 * index, area] + x_recv[index, part].astype(jnp.float32)
+        total[2 * index, area] = met
+        z_send[index, part] = met.astype(jnp.bfloat16)
+        z_copies[index, part] = remote(z_send.at[index, part], z_recv.at[1 - index, part], z1)
+        if number == 1:
+            fold_zz.wait_recv()
+            fold_own[...] = (
+                fold_3[high].astype(jnp.float32) + fold_4[...].astype(jnp.float32)
+            ).astype(jnp.bfloat16)
+            fold_local = local(fold_own, fold_rows(dp))
+            fold_y = remote(fold_own, fold_rows(dp), y1)
+            fold_x = remote(fold_own, fold_rows(dp), x1)
+        if number in (5, 7):
+            encode(*ready[count])
+            encode(*ready[count + 1])
+            count += 2
+    for entry in ready[count:]:
+        encode(*entry)
+
     fold_x.wait_recv()
     fold_d = remote(fold_rows(dp_x), fold_rows(dp_x), y1)
+
+    def pass_on(part):
+        onward[2, part].wait_recv()
+        onward[3, part] = remote(
+            encoded.at[2, area_of(0, part)], encoded.at[3, area_of(0, part)], z1
+        )
+        to_partner(2, part)
+
+    def gather(unit):
+        for part in range(parts):
+            pairs[unit, part].wait_recv()
+
+    pass_on(0)
+    pass_on(1)
+    pass_on(2)
+    fold_local.wait()
     fold_y.wait_recv()
     fold_d.wait_recv()
     scale = 1.0 / HEAD_DIM**0.5
@@ -728,30 +799,17 @@
 
         lax.fori_loop(0, queries.shape[0], one, 0)
 
-    for part in range(2):
-        pairs[0, part].wait_recv()
+    gather(0)
     attend(0, spot)
-
-    def pass_on(part):
-        onward[2, part].wait_recv()
-        onward[3, part] = remote(
-            encoded.at[2, area_of(0, part)], encoded.at[3, area_of(0, part)], z1
-        )
-        to_partner(2, part)
-
-    pass_on(0)
-    for part in range(2):
-        pairs[1, part].wait_recv()
+    pass_on(3)
+    gather(1)
     attend(1, spot_1)
-    pass_on(1)
-    for part in range(2):
-        pairs[2, part].wait_recv()
+    gather(2)
     attend(2, spot_2)
-    for part in range(2):
+    for part in range(parts):
         onward[3, part].wait_recv()
         to_partner(3, part)
-    for part in range(2):
-        pairs[3, part].wait_recv()
+    gather(3)
     attend(3, spot_3)
 
     text_at = lax.broadcasted_iota(jnp.int32, (text_rows, 1), 0)
@@ -855,21 +913,22 @@
     text_rows = text.shape[0]
     query_columns = q_weight.shape[1]
     pairs = query_columns // HEAD_DIM // 2
-    half = rows // 2
+    parts = 4
     token_rows = text_rows // lax.axis_size("mp")
     steps = o_weight.shape[1] // depth
     low, wide = jnp.bfloat16, jnp.float32
-    copies = 64 + 3 * steps
+    copies = 96 + 3 * steps
     scratch = [
         ((4, 2 * hidden, width), low),
         ((4, 2 * hidden, width), low),
         ((4, rows, width), low),
         ((4, rows, width), low),
         ((4, rows, width), wide),
-        ((2, 2, half, width), low),
-        ((2, 2, half, width), low),
-        ((2, 2, half, width), low),
-        ((2, 2, half, width), low),
+        ((2, 4, rows, 2 * hidden), low),
+        ((2, parts, rows // parts, width), low),
+        ((2, parts, rows // parts, width), low),
+        ((2, parts, rows // parts, width), low),
+        ((2, parts, rows // parts, width), low),
         ((4, 2 * rows, width), low),
         ((part_rows, depth), low),
         (kv.shape, low),

time: 158 us -> 152 us (0.962)
  Pallas kernels: 155 us -> 148 us
    pallas_call x1, Pallas kernels: 155 us -> 148 us  [fused(): pl.pallas_call(fused_kernel, out_shape=jax.ShapeDtypeStruct((token_rows,...]
where the time goes in v3:
time: 152 us; the launch traced here: 151 us
  Pallas kernels  148 us (97%)
  local copies, waits for them, and re-layouts  1.67 us (1%)
    pallas_call x1, Pallas kernels, fused(): pl.pallas_call(fused_kernel, out_shape=jax.ShapeDtypeStruct((token_rows,...  148 us

profile of v3, /device:TPU:0, one launch (start us, length us, event | category | flops | bytes accessed | tf_op | source)
XLA Modules:
  0.0 151.1 jit_solution(6608053372701661668)
XLA Ops:
  1.3 148.1 %fused.1 = bf16[16,8192]{1,0:T(8,128)(2,1)} custom-call(bf16[256,1280]{1,0:T(8,128)(2,1)} %bitcast.6, f32[1280]{0:T(1024)} %gain.1, bf16[160,1280]{1,0:T(8,128)(2,1)} %bitcast.7, bf16[160,1280]{1,0:T(8,128)(2,1)} %fc2.1, bf16[1280,1024]{1,0:T(8,128)(2,1)} %projector.1, bf16[1024,8,2,128]{3,2,1,0:T(2,128)(2,1)} %kv.1, bf16[128,8192]{1,0:T(8,128)(2,1)} %bitcast.4, ...), custom_call_target="tpu_custom_call" | custom-call | tf_op jit(solution)/shard_map/fused/pallas_call | solution.py:963
  149.4 1.7 %copy.15 = bf16[1,16,8192]{2,1,0:T(8,128)(2,1)} copy(bf16[1,16,8192]{2,1,0:T(8,128)(2,1)} %bitcast.5) | data formatting | bytes 524288

commit v4 on v3

--- a/solution.py
+++ b/solution.py
@@ -328,7 +328,7 @@
 
 def fused_kernel(
     image,
-    gain,
+    gain_from,
     fc1,
     fc2,
     projector,
@@ -336,8 +336,8 @@
     text,
     q_weight,
     o_weight,
-    tile_count,
-    text_start,
+    tiles_from,
+    start_from,
     out,
     up,
     down,
@@ -377,6 +377,11 @@
     o_2,
     o_3,
     o_4,
+    result,
+    gain,
+    tile_count,
+    text_start,
+    result_sem,
     local_sem,
     stage_sem,
     sends,
@@ -429,6 +434,11 @@
             stage_sem.at[slot],
         )
 
+    small_copies = [
+        local(gain_from, gain),
+        local(tiles_from, tile_count),
+        local(start_from, text_start),
+    ]
     image_copy = local(image, pixels.at[0])
     up_copy = local(fc1, up.at[0, pl.ds(0, hidden)])
     down_copy = local(fc2, down.at[0, pl.ds(0, hidden)])
@@ -462,12 +472,25 @@
     parts = x_send.shape[1]
     slim = rows // parts
     slices = [pl.ds(part * slim, slim) for part in range(parts)]
+    quarter = rows // 4
+    quarters = [pl.ds(begin, quarter) for begin in range(0, rows, quarter)]
     piece = 32
     bits = [pl.ds(begin, piece) for begin in range(0, hidden, piece)]
-    image_z = [remote(image.at[area], pixels.at[2, area], z1) for area in slices]
+    image_z, up_z, down_z = [], [], []
+    pieces = [(fc1, up, up_z, area) for area in bits]
+    pieces += [(fc2, down, down_z, area) for area in bits]
+
+    def image_out():
+        area = quarters[len(image_z)]
+        image_z.append(remote(image.at[area], pixels.at[2, area], z1))
+
+    for number, (source, target, group, area) in enumerate(pieces):
+        if number % 2 == 0 and len(image_z) < len(quarters):
+            image_out()
+        group.append(remote(source.at[area], target.at[2, area], z2))
+    while len(image_z) < len(quarters):
+        image_out()
     image_x = remote(image, pixels.at[1], x1)
-    up_z = [remote(fc1.at[area], up.at[2, area], z2) for area in bits]
-    down_z = [remote(fc2.at[area], down.at[2, area], z2) for area in bits]
     up_y = remote(fc1, up.at[1, mine], y1)
     down_y = remote(fc2, down.at[1, mine], y1)
     up_p = {0: remote(fc1, up.at[0, theirs], pc)}
@@ -553,6 +576,8 @@
 
         lax.fori_loop(0, last, one, 0)
 
+    for copy in small_copies:
+        copy.wait()
     image_copy.wait()
     up_copy.wait()
     down_copy.wait()
@@ -595,33 +620,37 @@
         copy.wait_recv()
         up_d.append(remote(up.at[2, bits[part]], up.at[3, bits[part]], y1))
     up_p[2] = remote(up.at[2, mine], up.at[2, theirs], pc)
-    image_d = []
+    image_d, shared = [], []
 
     def image_on(part):
         image_z[part].wait_recv()
-        image_d.append(remote(pixels.at[2, slices[part]], pixels.at[3, slices[part]], x1))
+        image_d.append(remote(pixels.at[2, quarters[part]], pixels.at[3, quarters[part]], x1))
 
     def down_on(part):
         down_z[part].wait_recv()
         down_d.append(remote(down.at[2, bits[part]], down.at[3, bits[part]], y1))
-
-    for part in range(parts - 1):
-        image_on(part)
+        mirror = pl.ds(hidden + part * piece, piece)
+        shared.append(remote(down.at[2, bits[part]], down.at[2, mirror], pc))
+
+    image_on(0)
+    image_on(1)
     up_p[1].wait_recv()
     down_p[1].wait_recv()
     mlp(1, False, 2, 0)
-    down_on(0)
+    image_on(2)
     up_p[2].wait_recv()
     widen(2, 2, 0)
-    image_on(parts - 1)
+    down_on(0)
+    image_on(3)
     down_on(1)
     normalise(2)
-    down_on(2)
     mlp(0, True, 1, 2)
     mlp(1, False, 1, 2)
-    for part in range(3, len(bits)):
+    for copy in up_d:
+        copy.wait_recv()
+    up_p[3] = remote(up.at[3, mine], up.at[3, theirs], pc)
+    for part in range(2, len(bits)):
         down_on(part)
-    down_p[2] = remote(down.at[2, mine], down.at[2, theirs], pc)
     fold_p.wait_recv()
     spots = fold_0.shape[0]
 
@@ -633,24 +662,29 @@
 
     lax.fori_loop(0, spots, fold_pair, 0)
     fold_z = remote(fold_1.at[:, 1 - low], fold_2, z1)
-    for copy in up_d:
-        copy.wait_recv()
-    up_p[3] = remote(up.at[3, mine], up.at[3, theirs], pc)
     up_p[3].wait_recv()
     widen(3, 1, 1)
-    down_p[2].wait_recv()
-    narrow(2, 1, 1)
     for copy in image_d:
         copy.wait_recv()
     normalise(3)
+    spread = []
+
+    def relay(part):
+        down_d[part].wait_recv()
+        mirror = pl.ds(hidden + part * piece, piece)
+        spread.append(remote(down.at[3, bits[part]], down.at[3, mirror], pc))
+
+    for part in range(2):
+        relay(part)
     mlp(0, True, 1, 3)
     mlp(1, False, 1, 3)
+    for part in range(2, len(bits)):
+        relay(part)
+    for copy in shared:
+        copy.wait_recv()
     widen(2, 1, 3)
-    spread = []
-    for part, copy in enumerate(down_d):
-        copy.wait_recv()
-        mirror = pl.ds(hidden + part * piece, piece)
-        spread.append(remote(down.at[3, bits[part]], down.at[3, mirror], pc))
+    narrow(2, 1, 3)
+    widen(3, 1, 3)
     for copy in spread:
         copy.wait_recv()
 
@@ -659,21 +693,19 @@
         x_send[index, part] = total[row, slices[part]].astype(jnp.bfloat16)
         return remote(x_send.at[index, part], x_recv.at[index, part], x1)
 
+    narrow(3, 1, 3)
+    x_copies = {(1, part): to_x(3, part) for part in range(parts)}
+    narrow(2, 1, 1)
     narrow(3, 1, 1)
-    x_copies = {(0, 0): to_x(1, 0), (0, 1): to_x(1, 1)}
-    widen(3, 1, 3)
-    narrow(2, 1, 3)
-    narrow(3, 1, 3)
-    order = [(0, 0), (0, 1)]
-    for part in range(2, parts):
-        order += [(1, part - 2), (0, part)]
-    order += [(1, part) for part in range(parts - 2, parts)]
-    for index, part in order[2:]:
-        x_copies[index, part] = to_x(2 * index + 1, part)
+    for part in range(parts):
+        x_copies[0, part] = to_x(1, part)
     widen(2, 1, 2)
-    widen(3, 2, 0, 2)
-    narrow(2, 2, 0, 2)
-    narrow(3, 2, 0, 2)
+    widen(3, 1, 2)
+    narrow(2, 1, 2)
+    narrow(3, 1, 2)
+    widen(3, 1, 0)
+    narrow(2, 1, 0)
+    narrow(3, 1, 0)
     fold_z.wait_recv()
     for index in range(2):
         fold_3[index] = (
@@ -687,37 +719,21 @@
     z_copies, pairs, onward = {}, {}, {}
 
     def area_of(core_side, part):
-        return pl.ds(core_side * rows + part * slim, slim)
+        group, inside = part // (parts // 2), part % (parts // 2)
+        return pl.ds(group * rows + core_side * (rows // 2) + inside * slim, slim)
 
     def to_partner(unit, part):
         pairs[unit, part] = remote(
             encoded.at[unit, area_of(0, part)], encoded.at[unit, area_of(1, part)], pc
         )
 
-    def encode(index, part):
-        z_copies[1 - index, part].wait_recv()
-        area = slices[part]
-        encoded[index, area_of(0, part)] = (
-            pixels[2 * index, area].astype(jnp.float32)
-            + total[2 * index, area]
-            + z_recv[index, part].astype(jnp.float32)
+    for part in range(parts):
+        x_copies[1, part].wait_recv()
+        z_send[part] = (
+            total[2, slices[part]] + x_recv[1, part].astype(jnp.float32)
         ).astype(jnp.bfloat16)
-        if index == 0:
-            onward[2, part] = remote(
-                encoded.at[0, area_of(0, part)], encoded.at[2, area_of(0, part)], z2
-            )
-        to_partner(index, part)
-
-    ready = [(index, part) for part in range(parts) for index in range(2)]
-    count = 0
-    for number, (index, part) in enumerate(order):
-        x_copies[index, part].wait_recv()
-        area = slices[part]
-        met = total[2 * index, area] + x_recv[index, part].astype(jnp.float32)
-        total[2 * index, area] = met
-        z_send[index, part] = met.astype(jnp.bfloat16)
-        z_copies[index, part] = remote(z_send.at[index, part], z_recv.at[1 - index, part], z1)
-        if number == 1:
+        z_copies[part] = remote(z_send.at[part], z_recv.at[part], z1)
+        if part == 1:
             fold_zz.wait_recv()
             fold_own[...] = (
                 fold_3[high].astype(jnp.float32) + fold_4[...].astype(jnp.float32)
@@ -725,54 +741,68 @@
             fold_local = local(fold_own, fold_rows(dp))
             fold_y = remote(fold_own, fold_rows(dp), y1)
             fold_x = remote(fold_own, fold_rows(dp), x1)
-        if number in (5, 7):
-            encode(*ready[count])
-            encode(*ready[count + 1])
-            count += 2
-    for entry in ready[count:]:
-        encode(*entry)
-
+    for part in range(parts):
+        x_copies[0, part].wait_recv()
+        z_copies[part].wait_recv()
+        area = slices[part]
+        encoded[0, area_of(0, part)] = (
+            pixels[0, area].astype(jnp.float32)
+            + total[0, area]
+            + x_recv[0, part].astype(jnp.float32)
+            + z_recv[part].astype(jnp.float32)
+        ).astype(jnp.bfloat16)
+        for unit, peer in ((2, z2), (1, z1)):
+            onward[unit, part] = remote(
+                encoded.at[0, area_of(0, part)], encoded.at[unit, area_of(0, part)], peer
+            )
+        to_partner(0, part)
     fold_x.wait_recv()
     fold_d = remote(fold_rows(dp_x), fold_rows(dp_x), y1)
 
     def pass_on(part):
+        onward[1, part].wait_recv()
+        to_partner(1, part)
         onward[2, part].wait_recv()
         onward[3, part] = remote(
             encoded.at[2, area_of(0, part)], encoded.at[3, area_of(0, part)], z1
         )
         to_partner(2, part)
 
-    def gather(unit):
-        for part in range(parts):
+    def gather(unit, begin=0, end=parts):
+        for part in range(begin, end):
             pairs[unit, part].wait_recv()
 
-    pass_on(0)
-    pass_on(1)
-    pass_on(2)
+    for part in range(parts // 2):
+        pass_on(part)
     fold_local.wait()
     fold_y.wait_recv()
     fold_d.wait_recv()
     scale = 1.0 / HEAD_DIM**0.5
     limit = tile_count[0] * TILE_TOK
 
-    def attend(unit, unit_spot):
-        count = 2 * rows
-        kv_block = jnp.dot(encoded[unit], folded[...], preferred_element_type=jnp.float32)
+    def attend(unit, unit_spot, begin=0, count=2 * rows):
+        area = pl.ds(0, count)
+        kv_block = jnp.dot(
+            encoded[unit, pl.ds(begin, count)], folded[...], preferred_element_type=jnp.float32
+        )
         key = kv_block[:, :HEAD_DIM]
         key_scale = lax.rsqrt(jnp.mean(key * key, axis=-1, keepdims=True) + 1e-06)
-        keys[...] = (key * key_scale).astype(jnp.bfloat16)
-        values[...] = kv_block[:, HEAD_DIM:].astype(jnp.bfloat16)
-        place = lax.broadcasted_iota(jnp.int32, (1, count), 1)
+        keys[area] = (key * key_scale).astype(jnp.bfloat16)
+        values[area] = kv_block[:, HEAD_DIM:].astype(jnp.bfloat16)
+        place = begin + lax.broadcasted_iota(jnp.int32, (1, count), 1)
+        group = jnp.where(place < rows, 0, 1)
+        inside = place - group * rows
+        mine_here = inside < rows // 2
         own_base = (unit_spot * CORES + core) * rows
-        other_base = (unit_spot * CORES + 1 - core) * rows - rows
-        token = place + jnp.where(place < rows, own_base, other_base)
+        other_base = (unit_spot * CORES + 1 - core) * rows - rows // 2
+        token = inside + group * (rows // 2) + jnp.where(mine_here, own_base, other_base)
         valid = token < limit
 
-        def one(group, carry):
+        def one(index, carry):
             scores = (
                 lax.dot_general(
-                    queries[group],
-                    keys[...],
+                    queries[index],
+                    keys[area],
                     (((1,), (1,)), ((), ())),
                     preferred_element_type=jnp.float32,
                 )
@@ -781,27 +811,28 @@
             scores = jnp.where(valid, scores, -1e30)
             top = jnp.max(scores, axis=-1, keepdims=True)
             if unit > 0:
-                before = tops[group][:, :1]
+                before = tops[index][:, :1]
                 top = jnp.maximum(before, top)
                 shrink = jnp.exp(before - top)
             weights = jnp.exp(scores - top)
             weight_sum = jnp.sum(weights, axis=-1, keepdims=True)
             blend = jnp.dot(
-                weights.astype(jnp.bfloat16), values[...], preferred_element_type=jnp.float32
+                weights.astype(jnp.bfloat16), values[area], preferred_element_type=jnp.float32
             )
             if unit > 0:
-                weight_sum += shrink * sums[group][:, :1]
-                blend += shrink * mixed[group]
-            tops[group] = jnp.broadcast_to(top, tops.shape[1:])
-            sums[group] = jnp.broadcast_to(weight_sum, sums.shape[1:])
-            mixed[group] = blend
+                weight_sum += shrink * sums[index][:, :1]
+                blend += shrink * mixed[index]
+            tops[index] = jnp.broadcast_to(top, tops.shape[1:])
+            sums[index] = jnp.broadcast_to(weight_sum, sums.shape[1:])
+            mixed[index] = blend
             return carry
 
         lax.fori_loop(0, queries.shape[0], one, 0)
 
     gather(0)
     attend(0, spot)
-    pass_on(3)
+    for part in range(parts // 2, parts):
+        pass_on(part)
     gather(1)
     attend(1, spot_1)
     gather(2)
@@ -883,11 +914,19 @@
 
     lax.fori_loop(0, steps, second, 0)
 
+    def result_copy(step):
+        return pltpu.make_async_copy(
+            result.at[step],
+            out.at[:, pl.ds(pl.multiple_of(step * depth, depth), depth)],
+            result_sem.at[step],
+        )
+
     def third(step, carry):
         o_third(step).wait_recv()
-        out[:, pl.ds(pl.multiple_of(step * depth, depth), depth)] = (
+        result[step] = (
             o_3[step, high].astype(jnp.float32) + o_4[step].astype(jnp.float32)
         ).astype(jnp.bfloat16)
+        result_copy(step).start()
         return carry
 
     lax.fori_loop(0, steps, third, 0)
@@ -898,6 +937,7 @@
         o_first(step).wait_send()
         o_second(step).wait_send()
         o_third(step).wait_send()
+        result_copy(step).wait()
         return carry
 
     lax.fori_loop(0, steps, drain, 0)
@@ -917,7 +957,7 @@
     token_rows = text_rows // lax.axis_size("mp")
     steps = o_weight.shape[1] // depth
     low, wide = jnp.bfloat16, jnp.float32
-    copies = 96 + 3 * steps
+    copies = 144 + 3 * steps
     scratch = [
         ((4, 2 * hidden, width), low),
         ((4, 2 * hidden, width), low),
@@ -927,8 +967,8 @@
         ((2, 4, rows, 2 * hidden), low),
         ((2, parts, rows // parts, width), low),
         ((2, parts, rows // parts, width), low),
-        ((2, parts, rows // parts, width), low),
-        ((2, parts, rows // parts, width), low),
+        ((parts, rows // parts, width), low),
+        ((parts, rows // parts, width), low),
         ((4, 2 * rows, width), low),
         ((part_rows, depth), low),
         (kv.shape, low),
@@ -957,16 +997,20 @@
         ((steps, 2, token_rows, depth), low),
         ((steps, 2, token_rows, depth), low),
         ((steps, token_rows, depth), low),
+        ((steps, token_rows, depth), low),
+        (gain.shape, wide),
     ]
-    vmem, anywhere = pl.BlockSpec(memory_space=pltpu.VMEM), pl.BlockSpec(memory_space=pl.ANY)
-    smem = pl.BlockSpec(memory_space=pltpu.SMEM)
+    anywhere = pl.BlockSpec(memory_space=pl.ANY)
     return pl.pallas_call(
         fused_kernel,
         out_shape=jax.ShapeDtypeStruct((token_rows, o_weight.shape[1]), jnp.bfloat16),
-        in_specs=[anywhere, vmem] + [anywhere] * 7 + [smem, smem],
-        out_specs=vmem,
+        in_specs=[anywhere] * 11,
+        out_specs=anywhere,
         scratch_shapes=[pltpu.VMEM(shape, kind) for shape, kind in scratch]
         + [
+            pltpu.SMEM(tile_count.shape, jnp.int32),
+            pltpu.SMEM(text_start.shape, jnp.int32),
+            pltpu.SemaphoreType.DMA((steps,)),
             pltpu.SemaphoreType.DMA((16,)),
             pltpu.SemaphoreType.DMA((4,)),
             pltpu.SemaphoreType.DMA((copies,)),

time: 152 us -> 147 us (0.967)
  Pallas kernels: 148 us -> 144 us
    pallas_call x1, Pallas kernels: 148 us -> 144 us  [fused(): pl.pallas_call(fused_kernel, out_shape=jax.ShapeDtypeStruct((token_rows,...]
where the time goes in v4:
time: 147 us
  Pallas kernels  144 us (98%)
  local copies, waits for them, and re-layouts  1.67 us (1%)
    pallas_call x1, Pallas kernels, fused(): pl.pallas_call(fused_kernel, out_shape=jax.ShapeDtypeStruct((token_rows,...  144 us

profile of v4, /device:TPU:0, one launch (start us, length us, event | category | flops | bytes accessed | tf_op | source)
XLA Modules:
  0.0 146.9 jit_solution(5673509629573811969)
XLA Ops:
  1.3 143.9 %fused.1 = bf16[16,8192]{1,0:T(8,128)(2,1)} custom-call(bf16[256,1280]{1,0:T(8,128)(2,1)} %bitcast.6, f32[1280]{0:T(1024)} %gain_from.1, bf16[160,1280]{1,0:T(8,128)(2,1)} %bitcast.7, bf16[160,1280]{1,0:T(8,128)(2,1)} %fc2.1, bf16[1280,1024]{1,0:T(8,128)(2,1)} %projector.1, bf16[1024,8,2,128]{3,2,1,0:T(2,128)(2,1)} %kv.1, bf16[128,8192]{1,0:T(8,128)(2,1)} %bitcast.4, ...), custom_call_target="tpu_custom_call" | custom-call | tf_op jit(solution)/shard_map/fused/pallas_call | solution.py:1004
  145.2 1.7 %copy.15 = bf16[1,16,8192]{2,1,0:T(8,128)(2,1)} copy(bf16[1,16,8192]{2,1,0:T(8,128)(2,1)} %bitcast.5) | data formatting | bytes 524288
